TPU v7x, 32 devices: a whole 2x2x4 slice. The times are simulated.
32 devices in a mesh: row: 4 (over z), col: 2 (over y), layer: 4 (over x, core).
Axes of the slice: x: 2, y: 2, z: 4, core: 2. Of those that a mesh axis runs over, the one named last changes fastest.
Arguments:
- amplitudes: float32 [2016, 73536], P('row', ('layer', 'col')), may hold values from -6 to 6
- integrals: float32 [73536, 768], P(('layer', 'col'), 'row'), may hold values from -0.03125 to 0.03125
- occ_energy: float32 [64], replicated, may hold values from -2 to -0.5
- vir_energy: float32 [384], replicated, may hold values from 0.2 to 3
Outputs:
- ladder: float32 [2016, 768], P('col', ('row', 'layer'))
- amplitude_step: float32 [2016, 768], P('col', ('row', 'layer'))
All inputs are finite; a program needn't handle non-finite values.
Results may differ from a plain program's by a relative error of at most 0.00007.
Values sent between devices are 32-bit elements; how exact they have to be, the bound alone decides.
A program may use at most 128 MiB of HBM per device.

v0:
```python
import jax
import jax.numpy as jnp
import numpy as np
from jax import lax
from jax.sharding import PartitionSpec as P


def lookup(indices, values_table):
    positions = jnp.arange(values_table.shape[0], dtype=jnp.int32)
    picked = jnp.where(indices[:, None] == positions[None, :], values_table[None, :], 0.0)
    return jnp.sum(picked, axis=1)


def owner_blocks(partial_sum):
    col_count = lax.axis_size("col")
    layer_count = lax.axis_size("layer")
    pair_rows = partial_sum.shape[0] // col_count
    slab_cols = partial_sum.shape[1] // layer_count
    blocks = partial_sum.reshape(col_count, pair_rows, layer_count, slab_cols)
    return blocks.transpose(0, 2, 1, 3).reshape(col_count * layer_count * pair_rows, slab_cols)


def contract(columns, rows):
    return lax.dot_general(
        columns,
        rows,
        (((1,), (1,)), ((), ())),
        precision=lax.Precision.HIGH,
        preferred_element_type=jnp.float32,
    )


def near_depth(depth):
    return -(-depth // (6 * 128)) * 128


def settled(value):
    return lax.optimization_barrier(value)


def halves(blocks, dim, upper, axis, swap):
    low_half = lax.index_in_dim(blocks, 0, dim, keepdims=False)
    high_half = lax.index_in_dim(blocks, 1, dim, keepdims=False)
    given = jnp.where(upper, low_half, high_half)
    return jnp.where(upper, high_half, low_half) + lax.ppermute(given, axis, swap)


def line_exchange(amplitudes, integrals):
    row = lax.axis_index("row")
    low = row < 2
    edge = (row == 0) | (row == 3)
    pair_rows = amplitudes.shape[0]
    depth, width = integrals.shape
    near = near_depth(depth)
    far = 2 * near
    columns = integrals.T
    parts = [0, far + near]
    firsts = [columns[:, start : start + far] for start in parts]
    up_pairs = [(0, 1), (1, 2), (2, 3)]
    down_pairs = [(3, 2), (2, 1), (1, 0)]

    def shift(up_payload, down_payload):
        return (
            lax.ppermute(up_payload, "row", up_pairs),
            lax.ppermute(down_payload, "row", down_pairs),
        )

    def sides(pair):
        up, down = pair
        return jnp.where(low, down, up), jnp.where(low, up, down)

    def kept(value):
        return jnp.where(edge, 0.0, value)

    hop1 = [shift(first, first) for first in firsts]
    seconds = []
    shared = []
    for start in parts:
        end = min(start + far + near, depth)
        pad = start + far + near - end
        seconds.append(jnp.pad(columns[:, start + far : end], ((0, 0), (0, pad))))
        shared.append(
            jnp.pad(amplitudes[:, start + far : end], ((0, 3 * width - pair_rows), (0, pad)))
        )
    hop2 = []
    for part in range(2):
        up1, down1 = hop1[part]
        edge2 = jnp.concatenate([seconds[part], shared[part][:width]], axis=1)
        hop2.append(
            shift(jnp.where(row == 0, edge2, up1), jnp.where(row == 3, edge2, down1))
        )
    hop3 = []
    for part in range(2):
        up2, down2 = hop2[part]
        edge3 = jnp.concatenate(
            [shared[part][width : 2 * width], shared[part][2 * width :]], axis=1
        )
        up_mid = jnp.concatenate([seconds[part], up2[:, :near]], axis=1)
        down_mid = jnp.concatenate([seconds[part], down2[:, :near]], axis=1)
        hop3.append(
            shift(
                jnp.where(row == 0, edge3, jnp.where(row == 1, up_mid, up2)),
                jnp.where(row == 3, edge3, jnp.where(row == 2, down_mid, down2)),
            )
        )
    own = settled(contract(columns, amplitudes))
    slot1 = slot2 = slot3 = extra1 = extra2 = extra3 = 0.0
    for part, start in enumerate(parts):
        rows_first = amplitudes[:, start : start + far]
        own_rows = shared[part][:pair_rows]
        inner1, outer1 = sides(hop1[part])
        slot1 += settled(contract(inner1, rows_first))
        third = settled(contract(outer1, rows_first))
        inner2, outer2 = sides(hop2[part])
        slot2 += settled(contract(inner2, rows_first))
        third = settled(third + contract(outer2[:, :near], own_rows))
        inner3, outer3 = sides(hop3[part])
        last = settled(contract(inner3, rows_first))
        slot3 += jnp.where(edge, last, third)
        columns3 = jnp.concatenate([inner3[:, :near], inner3[:, near:]], axis=0)
        columns3 = kept(columns3)
        mixed = settled(contract(columns3, own_rows))
        slot1 += mixed[:width]
        slot2 += mixed[width:]
        sent = jnp.concatenate([outer2[:, near:], outer3[:, :near], outer3[:, near:]], axis=0)
        sent = kept(sent[:pair_rows])
        three = settled(contract(jnp.concatenate([seconds[part], columns3], axis=0), sent))
        extra1 += three[:width]
        extra2 += three[width : 2 * width]
        extra3 += three[2 * width :]

    slots = [own, slot1, slot2, slot3]
    order = [jnp.where(edge, slots[at], slots[(at + 3) % 4]) for at in range(4)]
    extra = [jnp.zeros_like(extra1), extra1, extra2, extra3]
    both = [jnp.stack([order[at], extra[at]]) for at in range(4)]
    both = [jnp.where(low, both[at], both[3 - at]) for at in range(4)]
    layers = lax.axis_size("layer")
    slab = width // layers
    stacked = jnp.stack(both).reshape(2, 2, 2, 2, 2, slab, pair_rows)
    layer = lax.axis_index("layer")
    upper_col = lax.axis_index("col") == 1
    upper_pair = layer // 2 == 1
    pair_swap = [(0, 2), (2, 0), (1, 3), (3, 1)]
    core_swap = [(0, 1), (1, 0), (2, 3), (3, 2)]
    col_swap = [(0, 1), (1, 0)]
    halved = halves(stacked, 4, layer % 2 == 1, "layer", core_swap)
    pair_first = halves(halved[:, 0], 2, upper_pair, "layer", pair_swap)
    col_first = halves(halved[:, 1], 0, upper_col, "col", col_swap)
    mine = (
        halves(pair_first, 0, upper_col, "col", col_swap),
        halves(col_first, 1, upper_pair, "layer", pair_swap),
    )
    odd = row % 2 == 1
    same = jnp.where(odd, mine[1], mine[0])
    other = jnp.where(odd, mine[0], mine[1])
    same_pairs = []
    other_pairs = []
    for source_row in range(4):
        for source_col in range(2):
            bit = source_row % 2
            source = source_row * 2 + source_col
            same_pairs.append((source, (2 * source_col + bit) * 2 + source_row // 2))
            other_pairs.append((source, (2 * source_col + 1 - bit) * 2 + source_row // 2))
    same = lax.ppermute(same, ("row", "col"), same_pairs)
    other = lax.ppermute(other, ("row", "col"), other_pairs)
    even_rows = jnp.where(odd, other, same)
    odd_rows = jnp.where(odd, same, other)
    return jnp.concatenate([even_rows[0] + odd_rows[1], odd_rows[0] + even_rows[1]], axis=1)


def gathered(amplitudes, integrals):
    partial_rows = jnp.dot(
        amplitudes,
        lax.all_gather(integrals, "row", axis=1, tiled=True),
        precision=lax.Precision.HIGHEST,
        preferred_element_type=jnp.float32,
    )
    partial_sum = lax.all_to_all(partial_rows, "row", split_axis=1, concat_axis=0, tiled=True)
    return lax.psum_scatter(
        owner_blocks(partial_sum), ("col", "layer"), scatter_dimension=0, tiled=True
    )


def shards(amplitudes, integrals, occ_energy, vir_energy):
    in_line = lax.axis_size("row") == 4 and lax.axis_size("col") == 2
    in_line = in_line and lax.axis_size("layer") == 4
    fits = amplitudes.shape[0] <= 3 * integrals.shape[1]
    depth = integrals.shape[0]
    if in_line and fits and depth > 5 * near_depth(depth):
        ladder = line_exchange(amplitudes, integrals).T
    else:
        ladder = gathered(amplitudes, integrals)
    pair_rows = ladder.shape[0]
    slab_cols = ladder.shape[1]
    occupied = occ_energy.shape[0]
    virtuals = vir_energy.shape[0]
    first_np, second_np = np.triu_indices(occupied, 1)
    ij_start = lax.axis_index("col") * pair_rows
    ab_start = (
        lax.axis_index("row") * lax.axis_size("layer") + lax.axis_index("layer")
    ) * slab_cols
    first_index = lax.dynamic_slice_in_dim(
        jnp.asarray(first_np, dtype=jnp.int32), ij_start, pair_rows
    )
    second_index = lax.dynamic_slice_in_dim(
        jnp.asarray(second_np, dtype=jnp.int32), ij_start, pair_rows
    )
    pair_sum = lookup(first_index, occ_energy) + lookup(second_index, occ_energy)
    ab_index = ab_start + jnp.arange(slab_cols, dtype=jnp.int32)
    vir_sum = lookup(ab_index // virtuals, vir_energy) + lookup(ab_index % virtuals, vir_energy)
    denominator = pair_sum[:, None] - vir_sum[None, :]
    return (ladder, ladder / denominator)


def solution(mesh):
    in_specs = (P("row", ("layer", "col")), P(("layer", "col"), "row"), P(), P())
    out_specs = (P("col", ("row", "layer")), P("col", ("row", "layer")))
    return jax.shard_map(shards, mesh=mesh, in_specs=in_specs, out_specs=out_specs, check_vma=False)
```

profile of v0, /device:TPU:4, one launch (start us, length us, event | category | flops | bytes accessed | tf_op | source)
XLA Modules:
  0.0 388.0 jit_solution(13634472616881530810)
XLA Ops:
  0.6 5.2 %fusion.85 = (f32[192,3072]{1,0:T(8,128)}, f32[192,3072]{1,0:T(8,128)}) fusion(f32[192,9192]{1,0:T(8,128)} %bitcast.77), kind=kLoop, calls=%fused_computation.154 | loop fusion | bytes 9437184 | tf_op jit(solution)/shard_map/slice | solution.py:58
  5.9 4.9 %collective-permute-start.3 = (f32[192,3072]{1,0:T(8,128)}, f32[192,3072]{1,0:T(8,128)}, u32[]{:S(2)}, u32[]{:S(2)}) collective-permute-start(f32[192,3072]{1,0:T(8,128)} %get-tuple-element.19), channel_id=1, source_target_pairs={{0,8},{8,16},{16,24},{1,9},{9,17},{17,25},{2,10},{10,18},{18,26},{... | collective-permute-start | bytes 7077896 | tf_op jit(solution)/shard_map/ppermute | solution.py:64
  12.1 6.0 %collective-permute-start.9 = (f32[192,3072]{1,0:T(8,128)}, f32[192,3072]{1,0:T(8,128)}, u32[]{:S(2)}, u32[]{:S(2)}) collective-permute-start(f32[192,3072]{1,0:T(8,128)} %get-tuple-element.20), channel_id=1, source_target_pairs={{0,8},{8,16},{16,24},{1,9},{9,17},{17,25},{2,10},{10,18},{18,26},{... | collective-permute-start | bytes 7077896 | tf_op jit(solution)/shard_map/ppermute | solution.py:64
  19.3 12.9 %fusion.93 = f32[192,504]{1,0:T(8,128)} fusion(f32[9192,192]{0,1:T(8,128)S(1)} %copy-done.2, f32[504,9192]{1,0:T(8,128)} %param.6), kind=kOutput, calls=%fused_computation.162 | convolution fusion | flops 5336948736 | bytes 25977600 | tf_op jit(solution)/shard_map/dot_general | solution.py:24
  32.2 2.4 slice.242
  34.6 2.4 slice.247
  37.0 3.7 slice.194
  40.7 1.5 pad.15
  44.1 1.8 pad_slice_fusion.3
  45.8 3.6 fusion.84
  49.4 11.9 %collective-permute-done.3 = f32[192,3072]{1,0:T(8,128)} collective-permute-done((f32[192,3072]{1,0:T(8,128)}, f32[192,3072]{1,0:T(8,128)}, u32[]{:S(2)}, u32[]{:S(2)}) %collective-permute-start.3) | collective-permute-done | bytes 2359328 | tf_op jit(solution)/shard_map/ppermute | solution.py:64
  61.3 5.8 %collective-permute-done = f32[192,3072]{1,0:T(8,128)} collective-permute-done((f32[192,3072]{1,0:T(8,128)}, f32[192,3072]{1,0:T(8,128)}, u32[]{:S(2)}, u32[]{:S(2)}) %collective-permute-start) | collective-permute-done | bytes 2359328 | tf_op jit(solution)/shard_map/ppermute | solution.py:65
  67.1 2.5 fusion.48
  69.6 3.0 collective-permute-start.4
  73.9 37.9 %collective-permute-done.9 = f32[192,3072]{1,0:T(8,128)} collective-permute-done((f32[192,3072]{1,0:T(8,128)}, f32[192,3072]{1,0:T(8,128)}, u32[]{:S(2)}, u32[]{:S(2)}) %collective-permute-start.9) | collective-permute-done | bytes 2359328 | tf_op jit(solution)/shard_map/ppermute | solution.py:64
  111.8 5.8 %collective-permute-done.6 = f32[192,3072]{1,0:T(8,128)} collective-permute-done((f32[192,3072]{1,0:T(8,128)}, f32[192,3072]{1,0:T(8,128)}, u32[]{:S(2)}, u32[]{:S(2)}) %collective-permute-start.6) | collective-permute-done | bytes 2359328 | tf_op jit(solution)/shard_map/ppermute | solution.py:65
  117.7 4.6 %fusion.46 = (f32[192,3072]{1,0:T(8,128)}, f32[192,3072]{1,0:T(8,128)}) fusion(f32[192,3072]{1,0:T(8,128)} %collective-permute-done.9, f32[192,1536]{1,0:T(8,128)S(1)} %get-tuple-element.35, f32[192,1536]{1,0:T(8,128)S(1)} %pad.15, pred[]{:T(512)S(6)} %eq.49, f32[192,3072]{1,0:T(8,128)} %collective-permute-done.6, pred[]{:T(512)S(6)} %eq.96), kind=kLoop, calls=%fused_computation.64 | loop fusion | flops 1769472 | bytes 11796482 | tf_op jit(solution)/shard_map/jit(_where)/select_n | solution.py:90
  122.2 4.2 %collective-permute-start.10 = (f32[192,3072]{1,0:T(8,128)}, f32[192,3072]{1,0:T(8,128)}, u32[]{:S(2)}, u32[]{:S(2)}) collective-permute-start(f32[192,3072]{1,0:T(8,128)} %get-tuple-element.49), channel_id=1, source_target_pairs={{0,8},{8,16},{16,24},{1,9},{9,17},{17,25},{2,10},{10,18},{18,26},{... | collective-permute-start | bytes 7077896 | tf_op jit(solution)/shard_map/ppermute | solution.py:64
  126.5 1.7 collective-permute-start.7
  128.3 5.5 %fusion.8 = f32[192,504]{1,0:T(8,128)} fusion(f32[504,9192]{1,0:T(8,128)S(1)} %bitcast.72, f32[192,3072]{1,0:T(8,128)} %collective-permute-done, f32[192,3072]{1,0:T(8,128)} %collective-permute-done.3, pred[]{:T(512)S(6)} %lt.25), kind=kOutput, calls=%fused_computation.8 | convolution fusion | flops 1784217600 | bytes 11298817 | tf_op jit(solution)/shard_map/dot_general | solution.py:24
  133.7 5.4 %fusion.12 = f32[192,504]{1,0:T(8,128)} fusion(f32[504,9192]{1,0:T(8,128)S(1)} %bitcast.72, f32[192,3072]{1,0:T(8,128)} %collective-permute-done.3, f32[192,3072]{1,0:T(8,128)} %collective-permute-done, pred[]{:T(512)S(6)} %lt.25), kind=kOutput, calls=%fused_computation.12 | convolution fusion | flops 1784217600 | bytes 11298817 | tf_op jit(solution)/shard_map/dot_general | solution.py:24
  139.2 5.5 %fusion = f32[192,504]{1,0:T(8,128)} fusion(f32[504,9192]{1,0:T(8,128)S(1)} %bitcast.72, f32[192,3072]{1,0:T(8,128)} %collective-permute-done.6, f32[192,3072]{1,0:T(8,128)} %collective-permute-done.9, pred[]{:T(512)S(6)} %lt.25), kind=kOutput, calls=%fused_computation | convolution fusion | flops 1784217600 | bytes 11298817 | tf_op jit(solution)/shard_map/dot_general | solution.py:24
  144.7 5.5 %fusion.4 = f32[192,504]{1,0:T(8,128)} fusion(f32[504,9192]{1,0:T(8,128)S(1)} %bitcast.72, f32[192,3072]{1,0:T(8,128)} %collective-permute-done.9, f32[192,3072]{1,0:T(8,128)} %collective-permute-done.6, pred[]{:T(512)S(6)} %lt.25), kind=kOutput, calls=%fused_computation.4 | convolution fusion | flops 1784217600 | bytes 11298817 | tf_op jit(solution)/shard_map/dot_general | solution.py:24
  150.1 12.2 %collective-permute-done.4 = f32[192,3072]{1,0:T(8,128)S(1)} collective-permute-done((f32[192,3072]{1,0:T(8,128)S(1)}, f32[192,3072]{1,0:T(8,128)S(1)}, u32[]{:S(2)}, u32[]{:S(2)}) %collective-permute-start.4) | collective-permute-done | bytes 2359328 | tf_op jit(solution)/shard_map/ppermute | solution.py:64
  163.4 4.7 %collective-permute-done.1 = f32[192,3072]{1,0:T(8,128)S(1)} collective-permute-done((f32[192,3072]{1,0:T(8,128)S(1)}, f32[192,3072]{1,0:T(8,128)S(1)}, u32[]{:S(2)}, u32[]{:S(2)}) %collective-permute-start.1) | collective-permute-done | bytes 2359328 | tf_op jit(solution)/shard_map/ppermute | solution.py:65
  170.7 8.3 %fusion.39 = (f32[192,3072]{1,0:T(8,128)}, f32[192,3072]{1,0:T(8,128)}, f32[192,3072]{1,0:T(8,128)}) fusion(f32[192,3072]{1,0:T(8,128)} %copy-done.3, f32[192,1536]{1,0:T(8,128)} %slice.242, f32[192,1536]{1,0:T(8,128)} %slice.245, f32[192,1536]{1,0:T(8,128)} %pad_slice_fusion.4, f32[192,1536]{1,0:T(8,128)} %get-tuple-element.17, pred[]{:T(512)S(6)} %eq.98, ...), kind=kLoop, calls=%fused_computation.53 | loop fusion | flops 4718592 | bytes 17694724 | tf_op jit(solution)/shard_map/jit(_where)/select_n | solution.py:102
  179.0 3.7 collective-permute-start.5
  182.7 1.5 collective-permute-start.2
  184.3 7.4 %fusion.10 = f32[192,504]{1,0:T(8,128)} fusion(f32[504,9192]{1,0:T(8,128)} %param.6, f32[192,3072]{1,0:T(8,128)} %copy-done.4, f32[192,3072]{1,0:T(8,128)} %copy-done.3, pred[]{:T(512)S(6)} %lt.25), kind=kOutput, calls=%fused_computation.10 | convolution fusion | flops 1784217600 | bytes 11298817 | tf_op jit(solution)/shard_map/dot_general | solution.py:24
  192.8 1.5 fusion.55
  195.2 17.8 %collective-permute-done.10 = f32[192,3072]{1,0:T(8,128)} collective-permute-done((f32[192,3072]{1,0:T(8,128)}, f32[192,3072]{1,0:T(8,128)}, u32[]{:S(2)}, u32[]{:S(2)}) %collective-permute-start.10) | collective-permute-done | bytes 2359328 | tf_op jit(solution)/shard_map/ppermute | solution.py:64
  213.0 5.8 %collective-permute-done.7 = f32[192,3072]{1,0:T(8,128)} collective-permute-done((f32[192,3072]{1,0:T(8,128)}, f32[192,3072]{1,0:T(8,128)}, u32[]{:S(2)}, u32[]{:S(2)}) %collective-permute-start.7) | collective-permute-done | bytes 2359328 | tf_op jit(solution)/shard_map/ppermute | solution.py:65
  218.8 5.2 %fusion.2 = f32[192,504]{1,0:T(8,128)} fusion(f32[504,9192]{1,0:T(8,128)S(1)} %bitcast.74, f32[192,3072]{1,0:T(8,128)} %collective-permute-done.7, f32[192,3072]{1,0:T(8,128)} %collective-permute-done.10, pred[]{:T(512)S(6)} %lt.25), kind=kOutput, calls=%fused_computation.2 | convolution fusion | flops 1784217600 | bytes 11298817 | tf_op jit(solution)/shard_map/dot_general | solution.py:24
  224.0 2.4 slice.250
  226.4 2.4 slice.249
  228.8 8.3 %fusion.35 = (f32[192,3072]{1,0:T(8,128)}, f32[192,3072]{1,0:T(8,128)}, f32[192,3072]{1,0:T(8,128)}) fusion(f32[192,3072]{1,0:T(8,128)} %collective-permute-done.10, f32[192,1536]{1,0:T(8,128)} %copy-done.5, f32[192,1536]{1,0:T(8,128)} %slice.250, f32[192,1536]{1,0:T(8,128)} %get-tuple-element.34, f32[192,1536]{1,0:T(8,128)} %get-tuple-element.33, ...), kind=kLoop, calls=%fused_computation.49 | loop fusion | flops 4718592 | bytes 17694724 | tf_op jit(solution)/shard_map/jit(_where)/select_n | solution.py:102
  237.1 3.2 slice.262
  240.3 1.5 fusion.31
  242.6 3.4 collective-permute-start.11
  246.1 1.8 collective-permute-start.8
  247.8 15.7 %collective-permute-done.5 = f32[192,3072]{1,0:T(8,128)} collective-permute-done((f32[192,3072]{1,0:T(8,128)}, f32[192,3072]{1,0:T(8,128)}, u32[]{:S(2)}, u32[]{:S(2)}) %collective-permute-start.5) | collective-permute-done | bytes 2359328 | tf_op jit(solution)/shard_map/ppermute | solution.py:64
  263.5 5.8 %collective-permute-done.2 = f32[192,3072]{1,0:T(8,128)} collective-permute-done((f32[192,3072]{1,0:T(8,128)}, f32[192,3072]{1,0:T(8,128)}, u32[]{:S(2)}, u32[]{:S(2)}) %collective-permute-start.2) | collective-permute-done | bytes 2359328 | tf_op jit(solution)/shard_map/ppermute | solution.py:65
  269.3 3.0 broadcast_select_fusion.1
  272.4 2.8 fusion.14
  275.7 2.6 fusion.81
  278.3 4.0 %fusion.16 = f32[576,504]{1,0:T(8,128)} fusion(f32[384,1536]{1,0:T(8,128)S(1)} %maximum_select_fusion, f32[192,1536]{1,0:T(8,128)S(1)} %copy-done.8, f32[192,1536]{1,0:T(8,128)S(1)} %get-tuple-element.40, f32[192,1536]{1,0:T(8,128)S(1)} %get-tuple-element.39, f32[192,1536]{1,0:T(8,128)S(1)} %copy-done.26, pred[]{:T(512)S(6)} %or.3), kind=kOutput, calls=%fused_computation.20 | convolution fusion | flops 2678648832 | bytes 8239105 | tf_op jit(solution)/shard_map/dot_general | solution.py:24
  283.5 2.0 copy.28
  285.5 2.0 copy.30
  287.5 25.4 %collective-permute-done.11 = f32[192,3072]{1,0:T(8,128)} collective-permute-done((f32[192,3072]{1,0:T(8,128)}, f32[192,3072]{1,0:T(8,128)}, u32[]{:S(2)}, u32[]{:S(2)}) %collective-permute-start.11) | collective-permute-done | bytes 2359328 | tf_op jit(solution)/shard_map/ppermute | solution.py:64
  312.9 5.5 %collective-permute-done.8 = f32[192,3072]{1,0:T(8,128)} collective-permute-done((f32[192,3072]{1,0:T(8,128)}, f32[192,3072]{1,0:T(8,128)}, u32[]{:S(2)}, u32[]{:S(2)}) %collective-permute-start.8) | collective-permute-done | bytes 2359328 | tf_op jit(solution)/shard_map/ppermute | solution.py:65
  318.5 3.0 broadcast_select_fusion
  321.5 6.5 %fusion.6 = f32[192,504]{1,0:T(8,128)} fusion(f32[192,3072]{1,0:T(8,128)S(1)} %get-tuple-element.24, f32[504,9192]{1,0:T(8,128)} %param.6), kind=kOutput, calls=%fused_computation.6 | convolution fusion | flops 1783627776 | bytes 8939520 | tf_op jit(solution)/shard_map/dot_general | solution.py:24
  328.6 2.6 fusion.30
  331.2 4.0 %fusion.20 = f32[576,504]{1,0:T(8,128)} fusion(f32[384,1536]{1,0:T(8,128)S(1)} %maximum_select_fusion.1, f32[192,1536]{1,0:T(8,128)S(1)} %copy-done.6, f32[192,1536]{1,0:T(8,128)S(1)} %get-tuple-element.42, f32[192,1536]{1,0:T(8,128)S(1)} %get-tuple-element.41, f32[192,1536]{1,0:T(8,128)S(1)} %copy-done.25, pred[]{:T(512)S(6)} %or.3), kind=kOutput, calls=%fused_computation.24 | convolution fusion | flops 2678648832 | bytes 8239105 | tf_op jit(solution)/shard_map/dot_general | solution.py:24
  341.9 1.5 select_bitcast_fusion
  343.5 3.7 collective-permute-done.12
  347.2 2.0 bitcast_add_fusion
  350.0 1.5 collective-permute-start.13
  351.5 8.9 %collective-permute-done.15 = f32[2,2,48,504]{3,2,0,1:T(8,128)S(1)} collective-permute-done((f32[2,2,48,504]{3,2,0,1:T(8,128)S(1)}, f32[2,2,48,504]{3,2,0,1:T(8,128)S(1)}, u32[]{:S(2)}, u32[]{:S(2)}) %collective-permute-start.15) | collective-permute-done | bytes 387104 | tf_op jit(solution)/shard_map/ppermute | solution.py:45
  360.6 1.6 collective-permute-start.16
  363.1 3.7 collective-permute-done.16
  368.5 4.3 %collective-permute-start.18 = (f32[2,48,504]{2,1,0:T(8,128)S(1)}, f32[2,48,504]{2,1,0:T(8,128)S(1)}, u32[]{:S(2)}, u32[]{:S(2)}) collective-permute-start(f32[2,48,504]{2,1,0:T(8,128)S(1)} %get-tuple-element.8), channel_id=1, source_target_pairs={{0,0},{4,16},{8,8},{12,24},{16,4},{20,20},{24,12},{28,28},{1,1},{5... | collective-permute-start | bytes 580616 | tf_op jit(solution)/shard_map/ppermute | solution.py:164
  373.2 5.0 %collective-permute-done.17 = f32[2,48,504]{2,1,0:T(8,128)S(1)} collective-permute-done((f32[2,48,504]{2,1,0:T(8,128)S(1)}, f32[2,48,504]{2,1,0:T(8,128)S(1)}, u32[]{:S(2)}, u32[]{:S(2)}) %collective-permute-start.17) | collective-permute-done | bytes 193568 | tf_op jit(solution)/shard_map/ppermute | solution.py:165
  378.3 8.3 %collective-permute-done.18 = f32[2,48,504]{2,1,0:T(8,128)S(1)} collective-permute-done((f32[2,48,504]{2,1,0:T(8,128)S(1)}, f32[2,48,504]{2,1,0:T(8,128)S(1)}, u32[]{:S(2)}, u32[]{:S(2)}) %collective-permute-start.18) | collective-permute-done | bytes 193568 | tf_op jit(solution)/shard_map/ppermute | solution.py:164
  (148 shorter events, 25.9 us)
Async XLA Ops:
  0.6 18.7 %copy-start.2 = (f32[9192,192]{0,1:T(8,128)S(1)}, f32[9192,192]{0,1:T(8,128)}, u32[]{:S(2)}) copy-start(f32[9192,192]{0,1:T(8,128)} %param.7) | copy-start | bytes 21178372
  5.9 55.4 %collective-permute-start.3 = (f32[192,3072]{1,0:T(8,128)}, f32[192,3072]{1,0:T(8,128)}, u32[]{:S(2)}, u32[]{:S(2)}) collective-permute-start(f32[192,3072]{1,0:T(8,128)} %get-tuple-element.19), channel_id=1, source_target_pairs={{0,8},{8,16},{16,24},{1,9},{9,17},{17,25},{2,10},{10,18},{18,26},{... | collective-permute-start | bytes 7077896 | tf_op jit(solution)/shard_map/ppermute | solution.py:64
  10.8 56.3 %collective-permute-start = (f32[192,3072]{1,0:T(8,128)}, f32[192,3072]{1,0:T(8,128)}, u32[]{:S(2)}, u32[]{:S(2)}) collective-permute-start(f32[192,3072]{1,0:T(8,128)} %get-tuple-element.19), channel_id=1, source_target_pairs={{24,16},{16,8},{8,0},{25,17},{17,9},{9,1},{26,18},{18,10},{10,2},{... | collective-permute-start | bytes 7077896 | tf_op jit(solution)/shard_map/ppermute | solution.py:65
  12.1 99.8 %collective-permute-start.9 = (f32[192,3072]{1,0:T(8,128)}, f32[192,3072]{1,0:T(8,128)}, u32[]{:S(2)}, u32[]{:S(2)}) collective-permute-start(f32[192,3072]{1,0:T(8,128)} %get-tuple-element.20), channel_id=1, source_target_pairs={{0,8},{8,16},{16,24},{1,9},{9,17},{17,25},{2,10},{10,18},{18,26},{... | collective-permute-start | bytes 7077896 | tf_op jit(solution)/shard_map/ppermute | solution.py:64
  18.0 99.6 %collective-permute-start.6 = (f32[192,3072]{1,0:T(8,128)}, f32[192,3072]{1,0:T(8,128)}, u32[]{:S(2)}, u32[]{:S(2)}) collective-permute-start(f32[192,3072]{1,0:T(8,128)} %get-tuple-element.20), channel_id=1, source_target_pairs={{24,16},{16,8},{8,0},{25,17},{17,9},{9,1},{26,18},{18,10},{10,2},{... | collective-permute-start | bytes 7077896 | tf_op jit(solution)/shard_map/ppermute | solution.py:65
  40.7 2.2 slice-start.15
  40.7 3.4 copy-start
  42.9 74.7 %copy-start.5 = (f32[192,1536]{1,0:T(8,128)}, f32[192,1536]{1,0:T(8,128)S(1)}, u32[]{:S(2)}) copy-start(f32[192,1536]{1,0:T(8,128)S(1)} %pad.15) | copy-start | bytes 3538948
  42.9 85.3 %slice-start = ((s8[18579456]{0:T(1024)(128)(4,1)}), s8[4194304]{0:T(1024)(128)(4,1)S(1)}, s32[]{:S(2)}) async-start(s8[18579456]{0:T(1024)(128)(4,1)} %bitcast.71), calls=%async_computation | async-start | bytes 8388608
  44.1 84.2 %slice-start.1 = ((s8[18579456]{0:T(1024)(128)(4,1)}), s8[4194304]{0:T(1024)(128)(4,1)S(1)}, s32[]{:S(2)}) async-start(s8[18579456]{0:T(1024)(128)(4,1)} %bitcast.71), calls=%async_computation.1 | async-start | bytes 8388608
  45.8 21.3 %copy-start.7 = (f32[192,1536]{1,0:T(8,128)S(1)}, f32[192,1536]{1,0:T(8,128)}, u32[]{:S(2)}) copy-start(f32[192,1536]{1,0:T(8,128)} %slice.242) | copy-start | bytes 3538948
  67.1 61.1 %slice-start.2 = ((s8[18579456]{0:T(1024)(128)(4,1)}), s8[4194304]{0:T(1024)(128)(4,1)S(1)}, s32[]{:S(2)}) async-start(s8[18579456]{0:T(1024)(128)(4,1)} %bitcast.71), calls=%async_computation.2 | async-start | bytes 8388608
  67.1 61.1 %slice-start.3 = ((s8[18579456]{0:T(1024)(128)(4,1)}), s8[4194304]{0:T(1024)(128)(4,1)S(1)}, s32[]{:S(2)}) async-start(s8[18579456]{0:T(1024)(128)(4,1)} %bitcast.71), calls=%async_computation.3 | async-start | bytes 8388608
  69.6 92.7 %collective-permute-start.4 = (f32[192,3072]{1,0:T(8,128)S(1)}, f32[192,3072]{1,0:T(8,128)S(1)}, u32[]{:S(2)}, u32[]{:S(2)}) collective-permute-start(f32[192,3072]{1,0:T(8,128)S(1)} %get-tuple-element.45), channel_id=1, source_target_pairs={{0,8},{8,16},{16,24},{1,9},{9,17},{17,25},{2,10},{10,18},{18,26},{... | collective-permute-start | bytes 7077896 | tf_op jit(solution)/shard_map/ppermute | solution.py:64
  72.6 95.5 %collective-permute-start.1 = (f32[192,3072]{1,0:T(8,128)S(1)}, f32[192,3072]{1,0:T(8,128)S(1)}, u32[]{:S(2)}, u32[]{:S(2)}) collective-permute-start(f32[192,3072]{1,0:T(8,128)S(1)} %get-tuple-element.46), channel_id=1, source_target_pairs={{24,16},{16,8},{8,0},{25,17},{17,9},{9,1},{26,18},{18,10},{10,2},{... | collective-permute-start | bytes 7077896 | tf_op jit(solution)/shard_map/ppermute | solution.py:65
  117.7 10.6 %slice-start.4 = ((s8[18579456]{0:T(1024)(128)(4,1)}), s8[1802240]{0:T(1024)(128)(4,1)S(1)}, s32[]{:S(2)}) async-start(s8[18579456]{0:T(1024)(128)(4,1)} %bitcast.71), calls=%async_computation.4 | async-start | bytes 3604480
  122.2 90.7 %collective-permute-start.10 = (f32[192,3072]{1,0:T(8,128)}, f32[192,3072]{1,0:T(8,128)}, u32[]{:S(2)}, u32[]{:S(2)}) collective-permute-start(f32[192,3072]{1,0:T(8,128)} %get-tuple-element.49), channel_id=1, source_target_pairs={{0,8},{8,16},{16,24},{1,9},{9,17},{17,25},{2,10},{10,18},{18,26},{... | collective-permute-start | bytes 7077896 | tf_op jit(solution)/shard_map/ppermute | solution.py:64
  126.5 92.3 %collective-permute-start.7 = (f32[192,3072]{1,0:T(8,128)}, f32[192,3072]{1,0:T(8,128)}, u32[]{:S(2)}, u32[]{:S(2)}) collective-permute-start(f32[192,3072]{1,0:T(8,128)} %get-tuple-element.50), channel_id=1, source_target_pairs={{24,16},{16,8},{8,0},{25,17},{17,9},{9,1},{26,18},{18,10},{10,2},{... | collective-permute-start | bytes 7077896 | tf_op jit(solution)/shard_map/ppermute | solution.py:65
  162.3 8.4 %copy-start.3 = (f32[192,3072]{1,0:T(8,128)}, f32[192,3072]{1,0:T(8,128)S(1)}, u32[]{:S(2)}) copy-start(f32[192,3072]{1,0:T(8,128)S(1)} %collective-permute-done.4) | copy-start | bytes 7077892
  162.3 30.5 %slice-start.5 = ((s8[18579456]{0:T(1024)(128)(4,1)}), s8[1802240]{0:T(1024)(128)(4,1)S(1)}, s32[]{:S(2)}) async-start(s8[18579456]{0:T(1024)(128)(4,1)} %bitcast.73), calls=%async_computation.5 | async-start | bytes 3604480
  170.7 22.1 %slice-start.6 = ((s8[18579456]{0:T(1024)(128)(4,1)}), s8[4194304]{0:T(1024)(128)(4,1)S(1)}, s32[]{:S(2)}) async-start(s8[18579456]{0:T(1024)(128)(4,1)} %bitcast.73), calls=%async_computation.6 | async-start | bytes 8388608
  170.7 22.1 %slice-start.7 = ((s8[18579456]{0:T(1024)(128)(4,1)}), s8[4194304]{0:T(1024)(128)(4,1)S(1)}, s32[]{:S(2)}) async-start(s8[18579456]{0:T(1024)(128)(4,1)} %bitcast.73), calls=%async_computation.7 | async-start | bytes 8388608
  170.7 22.1 %slice-start.8 = ((s8[18579456]{0:T(1024)(128)(4,1)}), s8[4194304]{0:T(1024)(128)(4,1)S(1)}, s32[]{:S(2)}) async-start(s8[18579456]{0:T(1024)(128)(4,1)} %bitcast.73), calls=%async_computation.8 | async-start | bytes 8388608
  179.0 84.5 %collective-permute-start.5 = (f32[192,3072]{1,0:T(8,128)}, f32[192,3072]{1,0:T(8,128)}, u32[]{:S(2)}, u32[]{:S(2)}) collective-permute-start(f32[192,3072]{1,0:T(8,128)} %get-tuple-element.25), channel_id=1, source_target_pairs={{0,8},{8,16},{16,24},{1,9},{9,17},{17,25},{2,10},{10,18},{18,26},{... | collective-permute-start | bytes 7077896 | tf_op jit(solution)/shard_map/ppermute | solution.py:64
  182.7 9.0 %copy-start.9 = (f32[192,3072]{1,0:T(8,128)S(1)}, f32[192,3072]{1,0:T(8,128)}, u32[]{:S(2)}) copy-start(f32[192,3072]{1,0:T(8,128)} %get-tuple-element.27) | copy-start | bytes 7077892
  182.7 10.1 %slice-start.9 = ((s8[18579456]{0:T(1024)(128)(4,1)}), s8[4194304]{0:T(1024)(128)(4,1)S(1)}, s32[]{:S(2)}) async-start(s8[18579456]{0:T(1024)(128)(4,1)} %bitcast.73), calls=%async_computation.9 | async-start | bytes 8388608
  182.7 86.6 %collective-permute-start.2 = (f32[192,3072]{1,0:T(8,128)}, f32[192,3072]{1,0:T(8,128)}, u32[]{:S(2)}, u32[]{:S(2)}) collective-permute-start(f32[192,3072]{1,0:T(8,128)} %get-tuple-element.26), channel_id=1, source_target_pairs={{24,16},{16,8},{8,0},{25,17},{17,9},{9,1},{26,18},{18,10},{10,2},{... | collective-permute-start | bytes 7077896 | tf_op jit(solution)/shard_map/ppermute | solution.py:65
  192.8 1.5 copy-start.13
  228.8 11.5 %copy-start.1 = (f32[504,1512]{1,0:T(8,128)S(1)}, f32[504,1512]{1,0:T(8,128)}, u32[]{:S(2)}) copy-start(f32[504,1512]{1,0:T(8,128)} %slice.194) | copy-start | bytes 9144580
  228.8 43.5 %slice-start.10 = ((s8[18579456]{0:T(1024)(128)(4,1)}), s8[1802240]{0:T(1024)(128)(4,1)S(1)}, s32[]{:S(2)}) async-start(s8[18579456]{0:T(1024)(128)(4,1)} %bitcast.75), calls=%async_computation.10 | async-start | bytes 3604480
  228.8 43.5 %slice-start.11 = ((s8[18579456]{0:T(1024)(128)(4,1)}), s8[4194304]{0:T(1024)(128)(4,1)S(1)}, s32[]{:S(2)}) async-start(s8[18579456]{0:T(1024)(128)(4,1)} %bitcast.75), calls=%async_computation.11 | async-start | bytes 8388608
  228.8 43.5 %slice-start.12 = ((s8[18579456]{0:T(1024)(128)(4,1)}), s8[4194304]{0:T(1024)(128)(4,1)S(1)}, s32[]{:S(2)}) async-start(s8[18579456]{0:T(1024)(128)(4,1)} %bitcast.75), calls=%async_computation.12 | async-start | bytes 8388608
  237.1 3.2 copy-start.10
  240.3 1.5 copy-start.12
  240.3 32.1 %slice-start.13 = ((s8[18579456]{0:T(1024)(128)(4,1)}), s8[4194304]{0:T(1024)(128)(4,1)S(1)}, s32[]{:S(2)}) async-start(s8[18579456]{0:T(1024)(128)(4,1)} %bitcast.75), calls=%async_computation.13 | async-start | bytes 8388608
  242.6 70.3 %collective-permute-start.11 = (f32[192,3072]{1,0:T(8,128)}, f32[192,3072]{1,0:T(8,128)}, u32[]{:S(2)}, u32[]{:S(2)}) collective-permute-start(f32[192,3072]{1,0:T(8,128)} %get-tuple-element.28), channel_id=1, source_target_pairs={{0,8},{8,16},{16,24},{1,9},{9,17},{17,25},{2,10},{10,18},{18,26},{... | collective-permute-start | bytes 7077896 | tf_op jit(solution)/shard_map/ppermute | solution.py:64
  246.1 26.3 %slice-start.14 = ((s8[18579456]{0:T(1024)(128)(4,1)}), s8[4194304]{0:T(1024)(128)(4,1)S(1)}, s32[]{:S(2)}) async-start(s8[18579456]{0:T(1024)(128)(4,1)} %bitcast.75), calls=%async_computation.14 | async-start | bytes 8388608
  246.1 72.4 %collective-permute-start.8 = (f32[192,3072]{1,0:T(8,128)}, f32[192,3072]{1,0:T(8,128)}, u32[]{:S(2)}, u32[]{:S(2)}) collective-permute-start(f32[192,3072]{1,0:T(8,128)} %get-tuple-element.29), channel_id=1, source_target_pairs={{24,16},{16,8},{8,0},{25,17},{17,9},{9,1},{26,18},{18,10},{10,2},{... | collective-permute-start | bytes 7077896 | tf_op jit(solution)/shard_map/ppermute | solution.py:65
  275.7 2.6 copy-start.8
  275.7 2.6 copy-start.26
  328.5 2.6 copy-start.6
  328.5 2.6 copy-start.25
  335.1 2.1 copy-start.11
  335.1 2.1 copy-start.14
  335.1 2.1 copy-start.15
  335.4 3.4 copy-start.16
  335.4 3.4 copy-start.17
  336.3 2.4 copy-start.19
  337.3 1.5 copy-start.20
  337.3 1.7 copy-start.18
  337.3 1.7 copy-start.21
  337.3 1.7 copy-start.22
  339.0 1.6 copy-start.24
  343.5 3.8 collective-permute-start.12
  349.2 11.2 %collective-permute-start.15 = (f32[2,2,48,504]{3,2,0,1:T(8,128)S(1)}, f32[2,2,48,504]{3,2,0,1:T(8,128)S(1)}, u32[]{:S(2)}, u32[]{:S(2)}) collective-permute-start(f32[2,2,48,504]{3,2,0,1:T(8,128)S(1)} %select_bitcast_fusion.1), channel_id=1, source_target_pairs={{0,4},{4,0},{1,5},{5,1},{2,6},{6,2},{3,7},{7,3},{8,12},{12,8},{9,1... | collective-permute-start | bytes 1161224 | tf_op jit(solution)/shard_map/ppermute | solution.py:45
  350.0 12.9 %copy-start.28 = (s32[2016]{0:T(1024)S(1)}, s32[2016]{0:T(1024)}, u32[]{:S(2)}) copy-start(s32[2016]{0:T(1024)} %constant.77.clone) | copy-start | bytes 24196
  350.0 13.0 %copy-start.27 = (s32[2016]{0:T(1024)S(1)}, s32[2016]{0:T(1024)}, u32[]{:S(2)}) copy-start(s32[2016]{0:T(1024)} %constant.78.clone) | copy-start | bytes 24196
  350.0 12.2 %collective-permute-start.13 = (f32[2,2,48,504]{3,2,1,0:T(8,128)S(1)}, f32[2,2,48,504]{3,2,1,0:T(8,128)S(1)}, u32[]{:S(2)}, u32[]{:S(2)}) collective-permute-start(f32[2,2,48,504]{3,2,1,0:T(8,128)S(1)} %select_bitcast_fusion.2), channel_id=1, source_target_pairs={{0,2},{2,0},{1,3},{3,1},{4,6},{6,4},{5,7},{7,5},{8,10},{10,8},{9,1... | collective-permute-start | bytes 1161224 | tf_op jit(solution)/shard_map/ppermute | solution.py:45
  360.6 12.2 %copy-start.29 = (f32[384]{0:T(512)S(1)}, f32[384]{0:T(512)}, u32[]{:S(2)}) copy-start(f32[384]{0:T(512)} %param.9) | copy-start | bytes 4612
  360.6 12.4 %copy-start.30 = (f32[64]{0:T(128)S(1)}, f32[64]{0:T(128)}, u32[]{:S(2)}) copy-start(f32[64]{0:T(128)} %param.8) | copy-start | bytes 772
  360.6 6.2 %collective-permute-start.16 = (f32[2,48,504]{2,1,0:T(8,128)S(1)}, f32[2,48,504]{2,1,0:T(8,128)S(1)}, u32[]{:S(2)}, u32[]{:S(2)}) collective-permute-start(f32[2,48,504]{2,1,0:T(8,128)S(1)} %select_bitcast_fusion.7), channel_id=1, source_target_pairs={{0,2},{2,0},{1,3},{3,1},{4,6},{6,4},{5,7},{7,5},{8,10},{10,8},{9,1... | collective-permute-start | bytes 580616 | tf_op jit(solution)/shard_map/ppermute | solution.py:45
  362.3 5.9 %collective-permute-start.14 = (f32[2,48,504]{2,1,0:T(8,128)S(1)}, f32[2,48,504]{2,1,0:T(8,128)S(1)}, u32[]{:S(2)}, u32[]{:S(2)}) collective-permute-start(f32[2,48,504]{2,1,0:T(8,128)S(1)} %select_bitcast_fusion.8), channel_id=1, source_target_pairs={{0,4},{4,0},{1,5},{5,1},{2,6},{6,2},{3,7},{7,3},{8,12},{12,8},{9,1... | collective-permute-start | bytes 580616 | tf_op jit(solution)/shard_map/ppermute | solution.py:45
  368.3 9.9 %collective-permute-start.17 = (f32[2,48,504]{2,1,0:T(8,128)S(1)}, f32[2,48,504]{2,1,0:T(8,128)S(1)}, u32[]{:S(2)}, u32[]{:S(2)}) collective-permute-start(f32[2,48,504]{2,1,0:T(8,128)S(1)} %broadcast_select_fusion.9), channel_id=1, source_target_pairs={{0,8},{4,24},{8,0},{12,16},{16,12},{20,28},{24,4},{28,20},{1,9},{5... | collective-permute-start | bytes 580616 | tf_op jit(solution)/shard_map/ppermute | solution.py:165
  368.5 18.1 %collective-permute-start.18 = (f32[2,48,504]{2,1,0:T(8,128)S(1)}, f32[2,48,504]{2,1,0:T(8,128)S(1)}, u32[]{:S(2)}, u32[]{:S(2)}) collective-permute-start(f32[2,48,504]{2,1,0:T(8,128)S(1)} %get-tuple-element.8), channel_id=1, source_target_pairs={{0,0},{4,16},{8,8},{12,24},{16,4},{20,20},{24,12},{28,28},{1,1},{5... | collective-permute-start | bytes 580616 | tf_op jit(solution)/shard_map/ppermute | solution.py:164
  (2 other events, 2.7 us)
where the time goes:
time: 394 us; the launch traced here: 388 us
  waiting for transfers between devices  186 us (47%)
  matrix products  72.9 us (19%)
  local copies, waits for them, and re-layouts  45.2 us (11%)
  starting transfers between devices  42.9 us (11%)
  other arithmetic  39.6 us (10%)
    ppermute x6, waiting for transfers between devices, shift(): lax.ppermute(up_payload, 'row', up_pairs)  121 us
    dot_general x15, matrix products, contract(): lax.dot_general(columns, rows, (((1,), (1,)), ((), ())), precision=lax.Pr...  72.9 us
    ppermute x6, waiting for transfers between devices, shift(): lax.ppermute(down_payload, 'row', down_pairs)  33.5 us
    ppermute x6, starting transfers between devices, shift(): lax.ppermute(up_payload, 'row', up_pairs)  25.3 us
    ppermute x5, waiting for transfers between devices, halves(): lax.ppermute(given, axis, swap)  17.8 us
    select_n x2, other arithmetic, line_exchange(): jnp.where(row == 0, edge3, jnp.where(row == 1, up_mid, up2))  16.6 us
    ppermute x6, starting transfers between devices, shift(): lax.ppermute(down_payload, 'row', down_pairs)  8.9 us
    unnamed x96, local copies, waits for them, and re-layouts  8.79 us
  transfers between devices with their start and end apart: 19, of which 18 were waited for; matrix products, arithmetic and copies ran while one was open for 32% of the time, Pallas kernels for 0%

commit v1 on v0

v1 whole, which is shorter than its diff:
```python
import functools

import jax
import jax.numpy as jnp
import numpy as np
from jax import lax
from jax.experimental import pallas as pl
from jax.experimental.pallas import tpu as pltpu
from jax.sharding import PartitionSpec as P

MESH = pl.DeviceIdType.MESH
CHUNK = 384
PIECE = 16
LAG = 4


def lookup(indices, values_table):
    positions = jnp.arange(values_table.shape[0], dtype=jnp.int32)
    picked = jnp.where(indices[:, None] == positions[None, :], values_table[None, :], 0.0)
    return jnp.sum(picked, axis=1)


def owner_blocks(partial_sum):
    col_count = lax.axis_size("col")
    layer_count = lax.axis_size("layer")
    pair_rows = partial_sum.shape[0] // col_count
    slab_cols = partial_sum.shape[1] // layer_count
    blocks = partial_sum.reshape(col_count, pair_rows, layer_count, slab_cols)
    return blocks.transpose(0, 2, 1, 3).reshape(col_count * layer_count * pair_rows, slab_cols)


def split(value):
    high = value.astype(jnp.bfloat16)
    return high, (value - high.astype(jnp.float32)).astype(jnp.bfloat16)


def product(columns, rows):
    dims = (((1,), (1,)), ((), ()))

    def dot(left, right):
        return lax.dot_general(left, right, dims, preferred_element_type=jnp.float32)

    column_high, column_low = columns
    row_high, row_low = rows
    return (
        dot(column_low, row_high) + dot(column_high, row_low) + dot(column_high, row_high)
    )


def line_kernel(
    pair_rows,
    near,
    t_hbm,
    tail_hbm,
    v_hbm,
    out,
    rows,
    lent,
    land,
    acc,
    from_core,
    from_x,
    from_y,
    owned,
    load_sem,
    whole_sem,
    third_sem,
    lent_sem,
    sent_sem,
    hop_send,
    hop_recv,
    home_send,
    home_recv,
):
    chunks = land.shape[1]
    far = chunks - near
    thirds = acc.shape[1]
    group_rows = acc.shape[2]
    half_rows = group_rows // 2
    row = lax.axis_index("row")
    col = lax.axis_index("col")
    layer = lax.axis_index("layer")
    core = layer % 2
    x_side = layer // 2
    half = row // 2
    edge = (row == 0) | (row == 3)
    home = col == half
    edge_row = 3 * half
    inner_row = 1 + half
    far_inner = 2 - half
    far_edge = 3 - 3 * half
    core_mate = {"layer": x_side * 2 + (1 - core)}
    x_mate = {"layer": (1 - x_side) * 2 + core}
    y_mate = {"col": 1 - col}

    def remote(source, target, send_sem, recv_sem, device):
        return pltpu.make_async_remote_copy(
            src_ref=source,
            dst_ref=target,
            send_sem=send_sem,
            recv_sem=recv_sem,
            device_id=device,
            device_id_type=MESH,
        )

    def arrived(target, sem):
        pltpu.make_async_copy(target, target, sem).wait()

    def third_rows(third):
        return pl.ds(pl.multiple_of(third * group_rows, group_rows), group_rows)

    owned[...] = jnp.zeros_like(owned)
    barrier = pltpu.get_barrier_semaphore()
    for step in range(1, 4):
        pl.semaphore_signal(
            barrier, inc=1, device_id={"row": (row + step) % 4}, device_id_type=MESH
        )
    for mate in (core_mate, x_mate, y_mate):
        pl.semaphore_signal(barrier, inc=1, device_id=mate, device_id_type=MESH)
    rows_real = pl.ds(0, pair_rows)
    pl.semaphore_wait(barrier, 6)

    @pl.when(edge)
    def _():
        def send_far(i, carry):
            c = near + i
            remote(
                v_hbm.at[c], land.at[1, c], sent_sem.at[0], whole_sem.at[1, c],
                {"row": inner_row},
            ).start()
            return carry

        def send_lent(c, carry):
            start = pl.multiple_of(c * CHUNK, CHUNK)
            remote(
                t_hbm.at[:, pl.ds(start, CHUNK)], lent.at[c, rows_real], sent_sem.at[1],
                lent_sem.at[c], {"row": inner_row},
            ).start()
            return carry

        def send_near(n, carry):
            third, c = n // near, n % near
            remote(
                v_hbm.at[c, third_rows(third)], land.at[1, c, third_rows(third)],
                sent_sem.at[2], third_sem.at[0, n], {"row": inner_row},
            ).start()
            return carry

        lax.fori_loop(0, far, send_far, 0)
        lax.fori_loop(0, near, send_lent, 0)
        lax.fori_loop(0, near * thirds, send_near, 0)

    @pl.when(jnp.logical_not(edge))
    def _():
        def send_far(i, carry):
            c = near + i
            remote(
                v_hbm.at[c], land.at[2, c], sent_sem.at[0], whole_sem.at[2, c],
                {"row": far_inner},
            ).start()
            remote(
                v_hbm.at[c], land.at[1, c], sent_sem.at[1], whole_sem.at[1, c],
                {"row": edge_row},
            ).start()
            return carry

        def send_near(c, carry):
            remote(
                v_hbm.at[c], land.at[2, c], sent_sem.at[2], whole_sem.at[2, c],
                {"row": far_inner},
            ).start()
            return carry

        lax.fori_loop(0, far, send_far, 0)
        lax.fori_loop(0, near, send_near, 0)

    pltpu.make_async_copy(v_hbm, land.at[0], load_sem.at[0]).start()

    def load_rows(c, carry):
        start = pl.multiple_of(c * CHUNK, CHUNK)
        pltpu.make_async_copy(
            t_hbm.at[:, pl.ds(start, CHUNK)], rows.at[c, rows_real], load_sem.at[1]
        ).start()
        return carry

    lax.fori_loop(0, chunks - 1, load_rows, 0)
    pltpu.make_async_copy(
        tail_hbm, rows.at[chunks - 1, rows_real], load_sem.at[1]
    ).start()
    acc[...] = jnp.zeros_like(acc)
    spare = pl.ds(pair_rows, rows.shape[1] - pair_rows)

    def clear_rows(c, carry):
        rows[c, spare] = jnp.zeros_like(rows[c, spare])
        return carry

    def clear_lent(c, carry):
        lent[c, spare] = jnp.zeros_like(lent[c, spare])
        return carry

    lax.fori_loop(0, chunks, clear_rows, 0)
    lax.fori_loop(0, near, clear_lent, 0)
    arrived(land.at[0], load_sem.at[0])
    arrived(rows.at[:, rows_real], load_sem.at[1])

    def add_whole(block, c, pairs):
        other = split(block[c])
        for slot, part in pairs:
            sums = product(split(land[part, c]), other)
            acc[slot] += sums.reshape(acc.shape[1:])

    def add_third(block, c, third, pairs):
        other = split(block[c])
        for slot, part in pairs:
            acc[slot, third] += product(split(land[part, c, third_rows(third)]), other)

    half_mine = pl.ds(pl.multiple_of(core * half_rows, half_rows), half_rows)
    half_given = pl.ds(pl.multiple_of((1 - core) * half_rows, half_rows), half_rows)
    mine = pl.ds(pl.multiple_of(core * half_rows + x_side * PIECE, PIECE), PIECE)
    x_given = pl.ds(pl.multiple_of(core * half_rows + (1 - x_side) * PIECE, PIECE), PIECE)

    class Unit:
        def __init__(self, index, slots, group):
            self.index, self.slots, self.group = index, slots, group

        def core_copy(self):
            return remote(
                acc.at[self.slots, self.group, half_given],
                from_core.at[self.slots, self.group],
                hop_send.at[self.index, 0], hop_recv.at[self.index, 0], core_mate,
            )

        def x_copy(self):
            return remote(
                acc.at[self.slots, self.group, x_given],
                from_x.at[self.slots, self.group],
                hop_send.at[self.index, 1], hop_recv.at[self.index, 1], x_mate,
            )

        def y_copy(self):
            return remote(
                acc.at[self.slots, self.group, mine],
                from_y.at[self.slots, self.group],
                hop_send.at[self.index, 2], hop_recv.at[self.index, 2], y_mate,
            )

        def start(self):
            self.core_copy().start()

        def second(self):
            self.core_copy().wait()
            acc[self.slots, self.group, half_mine] += from_core[self.slots, self.group]
            self.x_copy().start()

        def third(self):
            self.x_copy().wait()
            acc[self.slots, self.group, mine] += from_x[self.slots, self.group]

            @pl.when(jnp.logical_not(home))
            def _():
                self.y_copy().start()

        def last(self, targets):
            @pl.when(jnp.logical_not(home))
            def _():
                self.y_copy().wait_send()

            @pl.when(home)
            def _():
                self.y_copy().wait_recv()
                acc[self.slots, self.group, mine] += from_y[self.slots, self.group]
                for slot, kind, device, send, recv in targets:
                    if device is None:
                        owned[kind, self.group] = acc[slot, self.group, mine]
                    else:
                        remote(
                            acc.at[slot, self.group, mine], owned.at[kind, self.group],
                            home_send.at[send], home_recv.at[recv], {"row": device},
                        ).start()

        def run(self, targets):
            self.start()
            self.second()
            self.third()
            self.last(targets)

    every = pl.ds(0, thirds)

    def kind_sem(kind, group):
        return kind * thirds + group

    @pl.when(edge)
    def _():
        def own(c, carry):
            add_whole(rows, c, ((0, 0),))
            return carry

        def other(part, i, carry):
            c = near + i
            arrived(land.at[part, c], whole_sem.at[part, c])
            add_whole(rows, c, ((part, part),))
            return carry

        lax.fori_loop(0, chunks, own, 0)
        lax.fori_loop(0, far, functools.partial(other, 1), 0)
        Unit(0, pl.ds(0, 2), every).run(
            ((0, 0, None, 0, 0), (1, 0, inner_row, 0, kind_sem(0, 0)))
        )
        lax.fori_loop(0, far, functools.partial(other, 2), 0)
        Unit(1, pl.ds(2, 1), every).run(((2, 0, far_inner, 1, kind_sem(0, 0)),))
        lax.fori_loop(0, far, functools.partial(other, 3), 0)
        Unit(2, pl.ds(3, 1), every).run(((3, 0, far_edge, 2, kind_sem(0, 0)),))

        @pl.when(home)
        def _():
            for send, slot in ((0, 1), (1, 2), (2, 3)):
                remote(
                    acc.at[slot, every, mine], owned.at[0, every],
                    home_send.at[send], home_recv.at[0], {"row": inner_row},
                ).wait_send()

        arrived_far = pl.ds(near, far)
        for at, source in (
            (0, land.at[0, arrived_far]), (2, land.at[0, pl.ds(0, near)]),
        ):
            remote(
                source, source, sent_sem.at[at], whole_sem.at[0, 0], {"row": inner_row}
            ).wait_send()
        remote(
            rows.at[pl.ds(0, near), rows_real], rows.at[pl.ds(0, near), rows_real],
            sent_sem.at[1], whole_sem.at[0, 0], {"row": inner_row},
        ).wait_send()

    @pl.when(jnp.logical_not(edge))
    def _():
        def first_far(i, carry):
            c = near + i
            arrived(land.at[1, c], whole_sem.at[1, c])
            remote(
                land.at[1, c], land.at[3, c], sent_sem.at[3], whole_sem.at[3, c],
                {"row": far_inner},
            ).start()
            arrived(land.at[2, c], whole_sem.at[2, c])
            remote(
                land.at[2, c], land.at[2, c], sent_sem.at[4], whole_sem.at[2, c],
                {"row": edge_row},
            ).start()
            add_whole(rows, c, ((0, 0), (4, 1), (1, 2)))
            return carry

        def first_near(c, carry):
            arrived(land.at[2, c], whole_sem.at[2, c])
            add_whole(rows, c, ((0, 0), (1, 2)))
            return carry

        def lent_chunk(c, carry):
            arrived(lent.at[c, rows_real], lent_sem.at[c])
            add_whole(lent, c, ((2, 0), (3, 2)))
            return carry

        def second_far(i, carry):
            c = near + i
            arrived(land.at[3, c], whole_sem.at[3, c])
            remote(
                land.at[3, c], land.at[3, c], sent_sem.at[5], whole_sem.at[3, c],
                {"row": edge_row},
            ).start()
            add_whole(rows, c, ((5, 3),))
            return carry

        lax.fori_loop(0, far, first_far, 0)
        early = near // 3

        def early_block(m, carry):
            lax.fori_loop(3 * m, 3 * m + 3, first_near, 0)
            return lent_chunk(m, carry)

        lax.fori_loop(0, early, early_block, 0)
        Unit(0, pl.ds(0, 2), every).run(
            ((0, 1, None, 0, 0), (1, 1, far_inner, 0, kind_sem(1, 0)))
        )
        late = near - early
        per = far // (late - 1)

        def late_block(m, carry):
            lax.fori_loop(per * m, per * m + per, second_far, 0)
            return lent_chunk(early + m, carry)

        lax.fori_loop(0, late - 1, late_block, 0)
        lax.fori_loop(per * (late - 1), far, second_far, 0)
        lent_chunk(near - 1, 0)

        lent_unit = Unit(1, pl.ds(2, 2), every)
        lent_targets = ((2, 2, None, 0, 0), (3, 2, far_inner, 1, kind_sem(2, 0)))

        def third_unit(third):
            return Unit(2 + third, pl.ds(4, 3), third)

        def third_targets(third):
            return (
                (4, 1, edge_row, 2 + third, kind_sem(1, third)),
                (5, 1, far_edge, 2 + thirds + third, kind_sem(1, third)),
                (6, 2, far_edge, 2 + 2 * thirds + third, kind_sem(2, third)),
            )

        pieces = near * thirds

        def pass_on(n):
            third, c = n // near, n % near
            arrived(land.at[1, c, third_rows(third)], third_sem.at[0, n])
            remote(
                land.at[1, c, third_rows(third)], land.at[3, c, third_rows(third)],
                sent_sem.at[6], third_sem.at[1, n], {"row": far_inner},
            ).start()

        def near_step(n, carry):
            third, c = n // near, n % near
            ahead = n + LAG

            @pl.when(ahead < pieces)
            def _():
                pass_on(ahead)

            add_third(rows, c, third, ((4, 1),))
            arrived(land.at[3, c, third_rows(third)], third_sem.at[1, n])
            add_third(rows, c, third, ((5, 3),))
            add_third(lent, c, third, ((6, 3),))

            first = third == 0
            before = third - 1

            def staged(at, on_lent, on_third):
                pl.when((c == at) & first)(on_lent)
                pl.when((c == at) & jnp.logical_not(first))(on_third)

            staged(1, lent_unit.start, lambda: third_unit(before).start())
            staged(3, lent_unit.second, lambda: third_unit(before).second())
            staged(5, lent_unit.third, lambda: third_unit(before).third())
            staged(
                7,
                lambda: lent_unit.last(lent_targets),
                lambda: third_unit(before).last(third_targets(before)),
            )
            return carry

        for n in range(LAG):
            pass_on(n)
        lax.fori_loop(0, pieces, near_step, 0)
        third_unit(thirds - 1).run(third_targets(thirds - 1))

        @pl.when(home)
        def _():
            sends = [(0, 1, every), (1, 3, every)]
            for at, slot in enumerate((4, 5, 6)):
                sends += [(2 + at * thirds + k, slot, k) for k in range(thirds)]
            for send, slot, group in sends:
                remote(
                    acc.at[slot, group, mine], owned.at[1, group],
                    home_send.at[send], home_recv.at[0], {"row": far_inner},
                ).wait_send()

        arrived_far = pl.ds(near, far)
        arrived_near = pl.ds(0, near)
        for at, source in (
            (0, land.at[0, arrived_far]),
            (1, land.at[0, arrived_far]),
            (2, land.at[0, arrived_near]),
            (3, land.at[1, arrived_far]),
            (4, land.at[2, arrived_far]),
            (5, land.at[3, arrived_far]),
            (6, land.at[1, arrived_near]),
        ):
            remote(
                source, source, sent_sem.at[at], whole_sem.at[0, 0], {"row": far_inner}
            ).wait_send()

    def owned_whole(kind):
        arrived(owned.at[kind, every], home_recv.at[kind_sem(kind, 0)])

    def owned_thirds(kind):
        for third in range(thirds):
            arrived(owned.at[kind, third], home_recv.at[kind_sem(kind, third)])

    @pl.when(edge & home)
    def _():
        owned_thirds(1)

    @pl.when(jnp.logical_not(edge) & home)
    def _():
        owned_whole(0)

    @pl.when(edge & jnp.logical_not(home))
    def _():
        owned_whole(0)
        owned_thirds(1)
        owned_thirds(2)

    @pl.when(jnp.logical_not(edge) & jnp.logical_not(home))
    def _():
        owned_whole(0)
        owned_whole(1)
        owned_whole(2)

    out[col] = owned[0] + owned[2]
    out[1 - col] = owned[1]


def line_exchange(amplitudes, integrals):
    pair_rows = amplitudes.shape[0]
    depth, width = integrals.shape
    chunks = -(-depth // CHUNK)
    near = 3 * chunks // 8
    layers = lax.axis_size("layer")
    thirds = width // (layers * PIECE)
    padded = -(-pair_rows // 128) * 128
    tail = jnp.pad(
        amplitudes[:, (chunks - 1) * CHUNK :], ((0, 0), (0, chunks * CHUNK - depth))
    )
    columns = jnp.pad(integrals, ((0, chunks * CHUNK - depth), (0, 0)))
    columns = columns.reshape(chunks, CHUNK, layers // 2, 2, thirds, PIECE)
    columns = columns.transpose(0, 4, 3, 2, 5, 1).reshape(chunks, width, CHUNK)
    group = width // thirds
    vmem = functools.partial(pltpu.VMEM, dtype=jnp.float32)
    dma = pltpu.SemaphoreType.DMA
    flops = 2 * 3 * 5 * pair_rows * depth * width
    out = pl.pallas_call(
        functools.partial(line_kernel, pair_rows, near),
        out_shape=jax.ShapeDtypeStruct((2, thirds, PIECE, padded), jnp.float32),
        in_specs=[pl.BlockSpec(memory_space=pl.ANY)] * 3,
        out_specs=pl.BlockSpec(memory_space=pltpu.VMEM),
        scratch_shapes=[
            vmem((chunks, padded, CHUNK)),
            vmem((near, padded, CHUNK)),
            vmem((4, chunks, width, CHUNK)),
            vmem((7, thirds, group, padded)),
            vmem((7, thirds, group // 2, padded)),
            vmem((7, thirds, PIECE, padded)),
            vmem((7, thirds, PIECE, padded)),
            vmem((3, thirds, PIECE, padded)),
            dma((2,)),
            dma((4, chunks)),
            dma((2, near * thirds)),
            dma((near,)),
            dma((7,)),
            dma((2 + thirds, 3)),
            dma((2 + thirds, 3)),
            dma((2 + 3 * thirds,)),
            dma((3 * thirds,)),
        ],
        compiler_params=pltpu.CompilerParams(
            collective_id=0, has_side_effects=True, vmem_limit_bytes=67043328
        ),
        cost_estimate=pl.CostEstimate(
            flops=flops, bytes_accessed=4 * depth * (pair_rows + width), transcendentals=0
        ),
    )(amplitudes, tail, columns)
    blocks = out.reshape(2, thirds * PIECE, padded)[:, :, :pair_rows]
    return blocks.transpose(0, 2, 1).reshape(2 * pair_rows, thirds * PIECE)


def gathered(amplitudes, integrals):
    partial_rows = jnp.dot(
        amplitudes,
        lax.all_gather(integrals, "row", axis=1, tiled=True),
        precision=lax.Precision.HIGHEST,
        preferred_element_type=jnp.float32,
    )
    partial_sum = lax.all_to_all(partial_rows, "row", split_axis=1, concat_axis=0, tiled=True)
    return lax.psum_scatter(
        owner_blocks(partial_sum), ("col", "layer"), scatter_dimension=0, tiled=True
    )


def fits_line(amplitudes, integrals):
    pair_rows = amplitudes.shape[0]
    depth, width = integrals.shape
    chunks = -(-depth // CHUNK)
    near = 3 * chunks // 8
    split_evenly = width % (4 * PIECE) == 0 and pair_rows % 8 == 0 and near % 3 == 0
    words = chunks * (4 * width + pair_rows) + near * pair_rows
    return split_evenly and near >= 9 and words * CHUNK * 4 < 56 * 2**20


def shards(amplitudes, integrals, occ_energy, vir_energy):
    in_line = lax.axis_size("row") == 4 and lax.axis_size("col") == 2
    in_line = in_line and lax.axis_size("layer") == 4
    if in_line and fits_line(amplitudes, integrals):
        ladder = line_exchange(amplitudes, integrals)
    else:
        ladder = gathered(amplitudes, integrals)
    pair_rows = ladder.shape[0]
    slab_cols = ladder.shape[1]
    occupied = occ_energy.shape[0]
    virtuals = vir_energy.shape[0]
    first_np, second_np = np.triu_indices(occupied, 1)
    ij_start = lax.axis_index("col") * pair_rows
    ab_start = (
        lax.axis_index("row") * lax.axis_size("layer") + lax.axis_index("layer")
    ) * slab_cols
    first_index = lax.dynamic_slice_in_dim(
        jnp.asarray(first_np, dtype=jnp.int32), ij_start, pair_rows
    )
    second_index = lax.dynamic_slice_in_dim(
        jnp.asarray(second_np, dtype=jnp.int32), ij_start, pair_rows
    )
    pair_sum = lookup(first_index, occ_energy) + lookup(second_index, occ_energy)
    ab_index = ab_start + jnp.arange(slab_cols, dtype=jnp.int32)
    vir_sum = lookup(ab_index // virtuals, vir_energy) + lookup(ab_index % virtuals, vir_energy)
    denominator = pair_sum[:, None] - vir_sum[None, :]
    return (ladder, ladder / denominator)


def solution(mesh):
    in_specs = (P("row", ("layer", "col")), P(("layer", "col"), "row"), P(), P())
    out_specs = (P("col", ("row", "layer")), P("col", ("row", "layer")))
    return jax.shard_map(shards, mesh=mesh, in_specs=in_specs, out_specs=out_specs, check_vma=False)
```

time: 394 us -> 357 us (0.906)
  Pallas kernels: 0 us -> 336 us
  waiting for transfers between devices: 186 us -> 0 us
  matrix products: 72.9 us -> 0 us
  starting transfers between devices: 42.9 us -> 0 us
  other arithmetic: 39.6 us -> 4.36 us
  local copies, waits for them, and re-layouts: 45.2 us -> 12.7 us
    pallas_call x0 -> x1, Pallas kernels: none -> 336 us  [line_exchange(): pl.pallas_call(functools.partial(line_kernel, pair_rows, near), out_shape...]
    ppermute x19 -> x0, waiting for transfers between devices: 186 us -> none  [the longest x6 121 us: shift(): lax.ppermute(up_payload, 'row', up_pairs)]
    dot_general x15 -> x0, matrix products: 72.9 us -> none  [contract(): lax.dot_general(columns, rows, (((1,), (1,)), ((), ())), precision=lax.Pr...]
    ppermute x19 -> x0, starting transfers between devices: 42.9 us -> none  [the longest x6 25.3 us: shift(): lax.ppermute(up_payload, 'row', up_pairs)]
    slice x20 -> x2, local copies, waits for them, and re-layouts: 34.7 us -> 0.01 us  [line_exchange(): amplitudes[:, (chunks - 1) * CHUNK:]]
    select_n x17 -> x0, other arithmetic: 31.9 us -> none  [the longest x2 16.6 us: line_exchange(): jnp.where(row == 0, edge3, jnp.where(row == 1, up_mid, up2))]
    unnamed x96 -> x3, local copies, waits for them, and re-layouts: 8.79 us -> 1.23 us
    reshape x0 -> x2, local copies, waits for them, and re-layouts: none -> 4.43 us  [the longest x1 4.19 us: line_exchange(): columns = columns.reshape(chunks, CHUNK, layers // 2, 2, thirds, PIECE)]
  transfers between devices with their start and end apart: 19 -> 0, of which waited for: 18 -> 0; matrix products, arithmetic and copies ran while one was open for 32% -> 0% of each run, Pallas kernels for 0% -> 0%
where the time goes in v1:
time: 357 us; the launch traced here: 354 us
  Pallas kernels  336 us (94%)
  local copies, waits for them, and re-layouts  12.7 us (4%)
  other arithmetic  4.36 us (1%)
    pallas_call x1, Pallas kernels, line_exchange(): pl.pallas_call(functools.partial(line_kernel, pair_rows, near), out_shape...  336 us

profile of v1, /device:TPU:4, one launch (start us, length us, event | category | flops | bytes accessed | tf_op | source)
XLA Modules:
  0.0 354.1 jit_solution(7476447076874385921)
XLA Ops:
  0.6 0.8 dynamic_slice.6
  1.4 0.8 dynamic_slice.7
  2.2 0.8 select_reduce_fusion
  3.0 0.6 add.54
  3.6 0.9 select_reduce_fusion.2
  4.5 0.6 add.59
  5.1 3.5 pad.9
  8.6 1.2 copy.12
  9.8 0.0 slice-start
  9.8 4.2 %copy.10 = f32[24,384,2,2,3,16]{1,5,2,3,4,0:T(8,128)} copy(f32[24,384,2,2,3,16]{1,0,5,4,3,2:T(8,128)S(1)} %bitcast.13) | data formatting | bytes 14155776 | tf_op jit(solution)/shard_map/reshape | solution.py:520
  14.0 0.0 slice-done
  14.0 0.9 pad.8.tail_hbm
  14.9 336.3 %shard_map.77 = f32[2,3,16,512]{3,2,1,0:T(8,128)} custom-call(f32[504,9192]{1,0:T(8,128)} %t_hbm.1, f32[504,384]{1,0:T(8,128)} %pad.8.tail_hbm, f32[24,192,384]{2,1,0:T(8,128)} %bitcast.15), custom_call_target="tpu_custom_call" | custom-call | flops 26684743680 | bytes 25590528 | tf_op jit(solution)/shard_map/pallas_call | solution.py:526
  351.3 0.9 slice_bitcast_fusion
  352.2 0.2 copy.11
  352.4 0.2 reshape.51
  352.6 0.0 copy-start
  352.6 1.5 subtract_divide_fusion
  354.1 0.0 copy-done
  (1 shorter events, 0.0 us)
Async XLA Ops:
  9.8 4.2 %slice-start = ((f32[504,9192]{1,0:T(8,128)}), f32[504,360]{1,0:T(8,128)S(1)}, s32[]{:S(2)}) async-start(f32[504,9192]{1,0:T(8,128)} %t_hbm.1), calls=%async_computation | async-start | bytes 1548288 | tf_op jit(solution)/shard_map/slice | solution.py:517
  352.6 1.5 copy-start

commit v2 on v1

--- a/solution.py
+++ b/solution.py
@@ -12,6 +12,7 @@
 CHUNK = 384
 PIECE = 16
 LAG = 4
+STAGES = 4
 
 
 def lookup(indices, values_table):
@@ -47,13 +48,58 @@
     )
 
 
+def denominators(pair_rows, occ, vir, below):
+    row = lax.axis_index("row")
+    col = lax.axis_index("col")
+    layer = lax.axis_index("layer")
+    blocks, slab, lanes = below.shape
+    occupied = occ.shape[0]
+    virtuals = vir.shape[0]
+    shape = (8, lanes)
+    block = lax.broadcasted_iota(jnp.int32, shape, 0)
+    pair = (blocks * col + block) * pair_rows + lax.broadcasted_iota(jnp.int32, shape, 1)
+
+    def begin(k):
+        return k * (2 * occupied - k - 1) // 2
+
+    def pick_first(k, carry):
+        energy, second = carry
+        inside = (pair >= begin(k)) & (pair < begin(k + 1))
+        return (
+            energy + jnp.where(inside, occ[k], 0.0),
+            jnp.where(inside, pair - begin(k) + k + 1, second),
+        )
+
+    zeros = jnp.zeros(shape, jnp.float32)
+    first_energy, second = lax.fori_loop(
+        0, occupied, pick_first, (zeros, jnp.zeros(shape, jnp.int32))
+    )
+
+    def pick_second(k, energy):
+        return energy + jnp.where(second == k, occ[k], 0.0)
+
+    pair_sum = first_energy + lax.fori_loop(0, occupied, pick_second, zeros)
+    start = (row * lax.axis_size("layer") + layer) * slab
+
+    def fill(i, carry):
+        index = start + i
+        vir_sum = jnp.full(shape, vir[index // virtuals]) + vir[index % virtuals]
+        value = pair_sum - vir_sum
+        for at in range(blocks):
+            below[at, pl.ds(i, 1)] = value[at : at + 1]
+        return carry
+
+    lax.fori_loop(0, slab, fill, 0)
+
+
 def line_kernel(
-    pair_rows,
     near,
     t_hbm,
-    tail_hbm,
     v_hbm,
+    occ_hbm,
+    vir_hbm,
     out,
+    step_out,
     rows,
     lent,
     land,
@@ -62,7 +108,14 @@
     from_x,
     from_y,
     owned,
+    relay,
+    stage,
+    below,
+    tail,
+    occ,
+    vir,
     load_sem,
+    stage_sem,
     whole_sem,
     third_sem,
     lent_sem,
@@ -71,7 +124,9 @@
     hop_recv,
     home_send,
     home_recv,
+    relay_recv,
 ):
+    pair_rows, depth = t_hbm.shape
     chunks = land.shape[1]
     far = chunks - near
     thirds = acc.shape[1]
@@ -109,27 +164,118 @@
     def third_rows(third):
         return pl.ds(pl.multiple_of(third * group_rows, group_rows), group_rows)
 
+    last_start = (chunks - 1) * CHUNK
+    last_depth = depth - last_start
+    rows_real = pl.ds(0, pair_rows)
+    spare = pl.ds(pair_rows, rows.shape[1] - pair_rows)
+
+    def chunk_at(j):
+        return jnp.where(j < far - 1, near + j, j - (far - 1))
+
+    def stage_copy(j):
+        start = pl.multiple_of(chunk_at(j) * CHUNK, CHUNK)
+        slot = j % STAGES
+        return pltpu.make_async_copy(
+            v_hbm.at[pl.ds(start, CHUNK)], stage.at[slot], stage_sem.at[slot]
+        )
+
+    last_stage = pltpu.make_async_copy(
+        v_hbm.at[pl.ds(last_start, last_depth)],
+        stage.at[STAGES, pl.ds(0, last_depth)],
+        stage_sem.at[STAGES],
+    )
+
+    def load_rows(c):
+        start = pl.multiple_of(c * CHUNK, CHUNK)
+        pltpu.make_async_copy(
+            t_hbm.at[:, pl.ds(start, CHUNK)], rows.at[c, rows_real], load_sem.at[0]
+        ).start()
+
+    barrier = pltpu.get_barrier_semaphore()
     owned[...] = jnp.zeros_like(owned)
-    barrier = pltpu.get_barrier_semaphore()
     for step in range(1, 4):
         pl.semaphore_signal(
             barrier, inc=1, device_id={"row": (row + step) % 4}, device_id_type=MESH
         )
     for mate in (core_mate, x_mate, y_mate):
         pl.semaphore_signal(barrier, inc=1, device_id=mate, device_id_type=MESH)
-    rows_real = pl.ds(0, pair_rows)
+    for j in range(STAGES):
+        stage_copy(j).start()
+    if last_depth < CHUNK:
+        lost = pl.ds(last_depth, CHUNK - last_depth)
+        stage[STAGES, lost] = jnp.zeros_like(stage[STAGES, lost])
+        rows[chunks - 1] = jnp.zeros_like(rows[chunks - 1])
+    last_stage.start()
+    last_rows = (
+        t_hbm.at[:, pl.ds(last_start, last_depth)],
+        tail,
+        load_sem.at[1],
+    )
+    slab = thirds * PIECE
+
+    def turn(slot, c):
+        turned = stage[slot].T
+        for third in range(thirds):
+            for at_core in range(2):
+                for at_x in range(2):
+                    source = (at_x * 2 + at_core) * slab + third * PIECE
+                    target = third * group_rows + at_core * half_rows + at_x * PIECE
+                    land[0, c, pl.ds(target, PIECE)] = turned[source : source + PIECE]
+
+    def prepare(j):
+        c = chunk_at(j)
+        stage_copy(j).wait()
+        turn(j % STAGES, c)
+
+        @pl.when(j + STAGES < chunks - 1)
+        def _():
+            stage_copy(j + STAGES).start()
+
+        load_rows(c)
+
+    def send_far(c):
+        @pl.when(edge)
+        def _():
+            remote(
+                land.at[0, c], land.at[1, c], sent_sem.at[0], whole_sem.at[1, c],
+                {"row": inner_row},
+            ).start()
+
+        @pl.when(jnp.logical_not(edge))
+        def _():
+            remote(
+                land.at[0, c], land.at[2, c], sent_sem.at[0], whole_sem.at[2, c],
+                {"row": far_inner},
+            ).start()
+            remote(
+                land.at[0, c], land.at[1, c], sent_sem.at[1], whole_sem.at[1, c],
+                {"row": edge_row},
+            ).start()
+
+    def send_near(c):
+        remote(
+            land.at[0, c], land.at[2, c], sent_sem.at[2], whole_sem.at[2, c],
+            {"row": far_inner},
+        ).start()
+
+    prepare(0)
     pl.semaphore_wait(barrier, 6)
+
+    def far_loop(j, carry):
+        prepare(j)
+        send_far(near + j - 1)
+        return carry
+
+    lax.fori_loop(1, far - 1, far_loop, 0)
+    last_stage.wait()
+    turn(STAGES, chunks - 1)
+    send_far(chunks - 2)
+    pltpu.make_async_copy(*last_rows).start()
+    prepare(far - 1)
+    send_far(chunks - 1)
 
     @pl.when(edge)
     def _():
-        def send_far(i, carry):
-            c = near + i
-            remote(
-                v_hbm.at[c], land.at[1, c], sent_sem.at[0], whole_sem.at[1, c],
-                {"row": inner_row},
-            ).start()
-            return carry
-
         def send_lent(c, carry):
             start = pl.multiple_of(c * CHUNK, CHUNK)
             remote(
@@ -138,57 +284,35 @@
             ).start()
             return carry
 
-        def send_near(n, carry):
+        lax.fori_loop(0, near, send_lent, 0)
+
+    def near_loop(c, carry):
+        prepare(far - 1 + c)
+        pl.when(jnp.logical_not(edge))(lambda: send_near(c - 1))
+        return carry
+
+    lax.fori_loop(1, near, near_loop, 0)
+    acc[...] = jnp.zeros_like(acc)
+
+    @pl.when(edge)
+    def _():
+        def send_piece(n, carry):
             third, c = n // near, n % near
             remote(
-                v_hbm.at[c, third_rows(third)], land.at[1, c, third_rows(third)],
+                land.at[0, c, third_rows(third)], land.at[1, c, third_rows(third)],
                 sent_sem.at[2], third_sem.at[0, n], {"row": inner_row},
             ).start()
             return carry
 
-        lax.fori_loop(0, far, send_far, 0)
-        lax.fori_loop(0, near, send_lent, 0)
-        lax.fori_loop(0, near * thirds, send_near, 0)
-
-    @pl.when(jnp.logical_not(edge))
-    def _():
-        def send_far(i, carry):
-            c = near + i
-            remote(
-                v_hbm.at[c], land.at[2, c], sent_sem.at[0], whole_sem.at[2, c],
-                {"row": far_inner},
-            ).start()
-            remote(
-                v_hbm.at[c], land.at[1, c], sent_sem.at[1], whole_sem.at[1, c],
-                {"row": edge_row},
-            ).start()
-            return carry
-
-        def send_near(c, carry):
-            remote(
-                v_hbm.at[c], land.at[2, c], sent_sem.at[2], whole_sem.at[2, c],
-                {"row": far_inner},
-            ).start()
-            return carry
-
-        lax.fori_loop(0, far, send_far, 0)
-        lax.fori_loop(0, near, send_near, 0)
-
-    pltpu.make_async_copy(v_hbm, land.at[0], load_sem.at[0]).start()
-
-    def load_rows(c, carry):
-        start = pl.multiple_of(c * CHUNK, CHUNK)
-        pltpu.make_async_copy(
-            t_hbm.at[:, pl.ds(start, CHUNK)], rows.at[c, rows_real], load_sem.at[1]
-        ).start()
-        return carry
-
-    lax.fori_loop(0, chunks - 1, load_rows, 0)
-    pltpu.make_async_copy(
-        tail_hbm, rows.at[chunks - 1, rows_real], load_sem.at[1]
-    ).start()
-    acc[...] = jnp.zeros_like(acc)
-    spare = pl.ds(pair_rows, rows.shape[1] - pair_rows)
+        lax.fori_loop(0, near * thirds, send_piece, 0)
+
+    pl.when(jnp.logical_not(edge))(lambda: send_near(near - 1))
+    energies = (
+        pltpu.make_async_copy(occ_hbm, occ, load_sem.at[2]),
+        pltpu.make_async_copy(vir_hbm, vir, load_sem.at[3]),
+    )
+    for copy in energies:
+        copy.start()
 
     def clear_rows(c, carry):
         rows[c, spare] = jnp.zeros_like(rows[c, spare])
@@ -198,10 +322,14 @@
         lent[c, spare] = jnp.zeros_like(lent[c, spare])
         return carry
 
-    lax.fori_loop(0, chunks, clear_rows, 0)
+    lax.fori_loop(0, chunks - 1, clear_rows, 0)
     lax.fori_loop(0, near, clear_lent, 0)
-    arrived(land.at[0], load_sem.at[0])
-    arrived(rows.at[:, rows_real], load_sem.at[1])
+    for copy in energies:
+        copy.wait()
+    denominators(pair_rows, occ, vir, below)
+    arrived(rows.at[pl.ds(0, chunks - 1), rows_real], load_sem.at[0])
+    pltpu.make_async_copy(*last_rows).wait()
+    rows[chunks - 1, rows_real, pl.ds(0, last_depth)] = tail[...]
 
     def add_whole(block, c, pairs):
         other = split(block[c])
@@ -220,8 +348,18 @@
     x_given = pl.ds(pl.multiple_of(core * half_rows + (1 - x_side) * PIECE, PIECE), PIECE)
 
     class Unit:
-        def __init__(self, index, slots, group):
+        def __init__(self, index, slots, group, here, there):
             self.index, self.slots, self.group = index, slots, group
+            self.here, self.there = here, there
+            self.slot_here, self.slot_there = here is not None, there is not None
+            if self.slot_here and self.slot_there:
+                self.kept = jnp.where(home, here, there)
+                self.given = jnp.where(home, there, here)
+                self.gives = self.takes = True
+            else:
+                self.kept = self.given = slots
+                self.takes = home if self.slot_here else jnp.logical_not(home)
+                self.gives = jnp.logical_not(self.takes)
 
         def core_copy(self):
             return remote(
@@ -239,8 +377,8 @@
 
         def y_copy(self):
             return remote(
-                acc.at[self.slots, self.group, mine],
-                from_y.at[self.slots, self.group],
+                acc.at[self.given, self.group, mine],
+                from_y.at[self.given, self.group],
                 hop_send.at[self.index, 2], hop_recv.at[self.index, 2], y_mate,
             )
 
@@ -255,39 +393,49 @@
         def third(self):
             self.x_copy().wait()
             acc[self.slots, self.group, mine] += from_x[self.slots, self.group]
-
-            @pl.when(jnp.logical_not(home))
-            def _():
-                self.y_copy().start()
-
-        def last(self, targets):
-            @pl.when(jnp.logical_not(home))
-            def _():
-                self.y_copy().wait_send()
-
-            @pl.when(home)
-            def _():
+            when(self.gives, lambda: self.y_copy().start())
+
+        def last(self, targets_here, targets_there=()):
+            when(self.gives, lambda: self.y_copy().wait_send())
+
+            def take():
                 self.y_copy().wait_recv()
-                acc[self.slots, self.group, mine] += from_y[self.slots, self.group]
-                for slot, kind, device, send, recv in targets:
+                acc[self.kept, self.group, mine] += from_y[self.kept, self.group]
+
+            when(self.takes, take)
+
+            def deliver(targets):
+                for slot, target, device, send, recv in targets:
+                    source = acc.at[slot, self.group, mine]
                     if device is None:
-                        owned[kind, self.group] = acc[slot, self.group, mine]
+                        target[self.group] = source[...]
                     else:
                         remote(
-                            acc.at[slot, self.group, mine], owned.at[kind, self.group],
-                            home_send.at[send], home_recv.at[recv], {"row": device},
+                            source, target.at[self.group], home_send.at[send], recv,
+                            {"row": device},
                         ).start()
 
-        def run(self, targets):
+            if targets_here:
+                pl.when(home)(lambda: deliver(targets_here))
+            if targets_there:
+                pl.when(jnp.logical_not(home))(lambda: deliver(targets_there))
+
+        def run(self, targets_here, targets_there=()):
             self.start()
             self.second()
             self.third()
-            self.last(targets)
+            self.last(targets_here, targets_there)
+
+    def when(condition, action):
+        if condition is True:
+            action()
+        else:
+            pl.when(condition)(action)
 
     every = pl.ds(0, thirds)
 
     def kind_sem(kind, group):
-        return kind * thirds + group
+        return home_recv.at[kind * thirds + group]
 
     @pl.when(edge)
     def _():
@@ -303,21 +451,35 @@
 
         lax.fori_loop(0, chunks, own, 0)
         lax.fori_loop(0, far, functools.partial(other, 1), 0)
-        Unit(0, pl.ds(0, 2), every).run(
-            ((0, 0, None, 0, 0), (1, 0, inner_row, 0, kind_sem(0, 0)))
+        Unit(0, pl.ds(0, 2), every, 0, None).run(
+            (
+                (0, owned.at[0], None, 0, None),
+                (1, owned.at[0], inner_row, 0, kind_sem(0, 0)),
+            )
         )
         lax.fori_loop(0, far, functools.partial(other, 2), 0)
-        Unit(1, pl.ds(2, 1), every).run(((2, 0, far_inner, 1, kind_sem(0, 0)),))
+        Unit(1, pl.ds(2, 1), every, None, 2).run(
+            (), ((2, relay.at[0], far_inner, 1, relay_recv.at[0]),)
+        )
         lax.fori_loop(0, far, functools.partial(other, 3), 0)
-        Unit(2, pl.ds(3, 1), every).run(((3, 0, far_edge, 2, kind_sem(0, 0)),))
+        Unit(2, pl.ds(3, 1), every, 3, None).run(
+            ((3, owned.at[0], far_edge, 2, kind_sem(0, 0)),)
+        )
+
+        def sent_home(send, group):
+            remote(
+                acc.at[0, group, mine], owned.at[0, group],
+                home_send.at[send], home_recv.at[0], {"row": inner_row},
+            ).wait_send()
 
         @pl.when(home)
         def _():
-            for send, slot in ((0, 1), (1, 2), (2, 3)):
-                remote(
-                    acc.at[slot, every, mine], owned.at[0, every],
-                    home_send.at[send], home_recv.at[0], {"row": inner_row},
-                ).wait_send()
+            sent_home(0, every)
+            sent_home(2, every)
+
+        @pl.when(jnp.logical_not(home))
+        def _():
+            sent_home(1, every)
 
         arrived_far = pl.ds(near, far)
         for at, source in (
@@ -376,8 +538,9 @@
             return lent_chunk(m, carry)
 
         lax.fori_loop(0, early, early_block, 0)
-        Unit(0, pl.ds(0, 2), every).run(
-            ((0, 1, None, 0, 0), (1, 1, far_inner, 0, kind_sem(1, 0)))
+        Unit(0, pl.ds(0, 2), every, 0, 1).run(
+            ((0, owned.at[1], None, 0, None),),
+            ((1, relay.at[1], far_inner, 0, relay_recv.at[1]),),
         )
         late = near - early
         per = far // (late - 1)
@@ -390,17 +553,25 @@
         lax.fori_loop(per * (late - 1), far, second_far, 0)
         lent_chunk(near - 1, 0)
 
-        lent_unit = Unit(1, pl.ds(2, 2), every)
-        lent_targets = ((2, 2, None, 0, 0), (3, 2, far_inner, 1, kind_sem(2, 0)))
-
-        def third_unit(third):
-            return Unit(2 + third, pl.ds(4, 3), third)
-
-        def third_targets(third):
+        lent_unit = Unit(1, pl.ds(2, 2), every, 2, 3)
+        lent_targets = (
+            ((2, owned.at[2], None, 0, None),),
+            ((3, relay.at[2], far_inner, 1, relay_recv.at[2]),),
+        )
+
+        def edge_unit(third):
+            return Unit(2 + third, pl.ds(4, 1), third, 4, None)
+
+        def edge_targets(third):
+            return ((4, owned.at[1], edge_row, 2 + third, kind_sem(1, third)),)
+
+        def last_unit(third):
+            return Unit(2 + thirds + third, pl.ds(5, 2), third, 5, None)
+
+        def last_targets(third):
             return (
-                (4, 1, edge_row, 2 + third, kind_sem(1, third)),
-                (5, 1, far_edge, 2 + thirds + third, kind_sem(1, third)),
-                (6, 2, far_edge, 2 + 2 * thirds + third, kind_sem(2, third)),
+                (5, owned.at[1], far_edge, 2 + thirds + third, kind_sem(1, third)),
+                (6, owned.at[2], far_edge, 2 + 2 * thirds + third, kind_sem(2, third)),
             )
 
         pieces = near * thirds
@@ -412,52 +583,83 @@
                 land.at[1, c, third_rows(third)], land.at[3, c, third_rows(third)],
                 sent_sem.at[6], third_sem.at[1, n], {"row": far_inner},
             ).start()
+            add_third(rows, c, third, ((4, 1),))
 
         def near_step(n, carry):
             third, c = n // near, n % near
-            ahead = n + LAG
-
-            @pl.when(ahead < pieces)
+
+            @pl.when(n + LAG < pieces)
             def _():
-                pass_on(ahead)
-
-            add_third(rows, c, third, ((4, 1),))
+                pass_on(n + LAG)
+
             arrived(land.at[3, c, third_rows(third)], third_sem.at[1, n])
             add_third(rows, c, third, ((5, 3),))
             add_third(lent, c, third, ((6, 3),))
 
             first = third == 0
+            later = jnp.logical_not(first)
             before = third - 1
-
-            def staged(at, on_lent, on_third):
-                pl.when((c == at) & first)(on_lent)
-                pl.when((c == at) & jnp.logical_not(first))(on_third)
-
-            staged(1, lent_unit.start, lambda: third_unit(before).start())
-            staged(3, lent_unit.second, lambda: third_unit(before).second())
-            staged(5, lent_unit.third, lambda: third_unit(before).third())
-            staged(
-                7,
-                lambda: lent_unit.last(lent_targets),
-                lambda: third_unit(before).last(third_targets(before)),
+            pl.when(first & (c == 1))(lent_unit.start)
+            pl.when(first & (c == 3))(lent_unit.second)
+            pl.when(first & (c == 5))(lent_unit.third)
+            pl.when(first & (c == 7))(lambda: lent_unit.last(*lent_targets))
+            pl.when(later & (c == 1))(lambda: last_unit(before).start())
+            pl.when(later & (c == 3))(lambda: last_unit(before).second())
+            pl.when(later & (c == 5))(lambda: last_unit(before).third())
+            pl.when(later & (c == 7))(
+                lambda: last_unit(before).last(last_targets(before))
+            )
+            pl.when(c == near - LAG)(lambda: edge_unit(third).start())
+            pl.when(c == near - LAG + 2)(lambda: edge_unit(third).second())
+            pl.when(later & (c == 0))(lambda: edge_unit(before).third())
+            pl.when(later & (c == 2))(
+                lambda: edge_unit(before).last(edge_targets(before))
             )
             return carry
+
+        def send_relay(kind):
+            return remote(
+                relay.at[kind], owned.at[kind], home_send.at[2 + 3 * thirds + kind],
+                kind_sem(kind, 0), y_mate,
+            )
+
+        def relay_on(kind):
+            @pl.when(home)
+            def _():
+                arrived(relay.at[kind], relay_recv.at[kind])
+                send_relay(kind).start()
 
         for n in range(LAG):
             pass_on(n)
         lax.fori_loop(0, pieces, near_step, 0)
-        third_unit(thirds - 1).run(third_targets(thirds - 1))
+        final = thirds - 1
+        last_unit(final).start()
+        edge_unit(final).third()
+        relay_on(1)
+        last_unit(final).second()
+        edge_unit(final).last(edge_targets(final))
+        relay_on(2)
+        last_unit(final).third()
+        last_unit(final).last(last_targets(final))
+        relay_on(0)
+
+        def sent_home(send, group):
+            remote(
+                acc.at[0, group, mine], owned.at[1, group],
+                home_send.at[send], home_recv.at[0], {"row": far_inner},
+            ).wait_send()
 
         @pl.when(home)
         def _():
-            sends = [(0, 1, every), (1, 3, every)]
-            for at, slot in enumerate((4, 5, 6)):
-                sends += [(2 + at * thirds + k, slot, k) for k in range(thirds)]
-            for send, slot, group in sends:
-                remote(
-                    acc.at[slot, group, mine], owned.at[1, group],
-                    home_send.at[send], home_recv.at[0], {"row": far_inner},
-                ).wait_send()
+            for send in range(2, 2 + 3 * thirds):
+                sent_home(send, 0)
+            for kind in range(3):
+                send_relay(kind).wait_send()
+
+        @pl.when(jnp.logical_not(home))
+        def _():
+            sent_home(0, every)
+            sent_home(1, every)
 
         arrived_far = pl.ds(near, far)
         arrived_near = pl.ds(0, near)
@@ -475,11 +677,11 @@
             ).wait_send()
 
     def owned_whole(kind):
-        arrived(owned.at[kind, every], home_recv.at[kind_sem(kind, 0)])
+        arrived(owned.at[kind, every], kind_sem(kind, 0))
 
     def owned_thirds(kind):
         for third in range(thirds):
-            arrived(owned.at[kind, third], home_recv.at[kind_sem(kind, third)])
+            arrived(owned.at[kind, third], kind_sem(kind, third))
 
     @pl.when(edge & home)
     def _():
@@ -501,33 +703,32 @@
         owned_whole(1)
         owned_whole(2)
 
-    out[col] = owned[0] + owned[2]
-    out[1 - col] = owned[1]
-
-
-def line_exchange(amplitudes, integrals):
+    for block, value in ((col, owned[0] + owned[2]), (1 - col, owned[1])):
+        ladder = value.reshape(out.shape[1:])
+        out[block] = ladder
+        step_out[block] = ladder / below[block]
+
+
+def line_exchange(amplitudes, integrals, occ_energy, vir_energy):
     pair_rows = amplitudes.shape[0]
     depth, width = integrals.shape
     chunks = -(-depth // CHUNK)
     near = 3 * chunks // 8
     layers = lax.axis_size("layer")
-    thirds = width // (layers * PIECE)
+    slab = width // layers
+    thirds = slab // PIECE
     padded = -(-pair_rows // 128) * 128
-    tail = jnp.pad(
-        amplitudes[:, (chunks - 1) * CHUNK :], ((0, 0), (0, chunks * CHUNK - depth))
-    )
-    columns = jnp.pad(integrals, ((0, chunks * CHUNK - depth), (0, 0)))
-    columns = columns.reshape(chunks, CHUNK, layers // 2, 2, thirds, PIECE)
-    columns = columns.transpose(0, 4, 3, 2, 5, 1).reshape(chunks, width, CHUNK)
     group = width // thirds
     vmem = functools.partial(pltpu.VMEM, dtype=jnp.float32)
+    smem = functools.partial(pltpu.SMEM, dtype=jnp.float32)
     dma = pltpu.SemaphoreType.DMA
     flops = 2 * 3 * 5 * pair_rows * depth * width
-    out = pl.pallas_call(
-        functools.partial(line_kernel, pair_rows, near),
-        out_shape=jax.ShapeDtypeStruct((2, thirds, PIECE, padded), jnp.float32),
-        in_specs=[pl.BlockSpec(memory_space=pl.ANY)] * 3,
-        out_specs=pl.BlockSpec(memory_space=pltpu.VMEM),
+    block = jax.ShapeDtypeStruct((2, slab, padded), jnp.float32)
+    results = pl.pallas_call(
+        functools.partial(line_kernel, near),
+        out_shape=(block, block),
+        in_specs=[pl.BlockSpec(memory_space=pl.ANY)] * 4,
+        out_specs=[pl.BlockSpec(memory_space=pltpu.VMEM)] * 2,
         scratch_shapes=[
             vmem((chunks, padded, CHUNK)),
             vmem((near, padded, CHUNK)),
@@ -537,15 +738,23 @@
             vmem((7, thirds, PIECE, padded)),
             vmem((7, thirds, PIECE, padded)),
             vmem((3, thirds, PIECE, padded)),
-            dma((2,)),
+            vmem((3, thirds, PIECE, padded)),
+            vmem((STAGES + 1, CHUNK, width)),
+            vmem((2, slab, padded)),
+            vmem((pair_rows, depth - (chunks - 1) * CHUNK)),
+            smem(occ_energy.shape),
+            smem(vir_energy.shape),
+            dma((4,)),
+            dma((STAGES + 1,)),
             dma((4, chunks)),
             dma((2, near * thirds)),
             dma((near,)),
             dma((7,)),
-            dma((2 + thirds, 3)),
-            dma((2 + thirds, 3)),
-            dma((2 + 3 * thirds,)),
+            dma((2 + 2 * thirds, 3)),
+            dma((2 + 2 * thirds, 3)),
+            dma((5 + 3 * thirds,)),
             dma((3 * thirds,)),
+            dma((3,)),
         ],
         compiler_params=pltpu.CompilerParams(
             collective_id=0, has_side_effects=True, vmem_limit_bytes=67043328
@@ -553,9 +762,12 @@
         cost_estimate=pl.CostEstimate(
             flops=flops, bytes_accessed=4 * depth * (pair_rows + width), transcendentals=0
         ),
-    )(amplitudes, tail, columns)
-    blocks = out.reshape(2, thirds * PIECE, padded)[:, :, :pair_rows]
-    return blocks.transpose(0, 2, 1).reshape(2 * pair_rows, thirds * PIECE)
+    )(amplitudes, integrals, occ_energy, vir_energy)
+
+    def placed(value):
+        return value[:, :, :pair_rows].transpose(0, 2, 1).reshape(2 * pair_rows, slab)
+
+    return tuple(placed(value) for value in results)
 
 
 def gathered(amplitudes, integrals):
@@ -585,9 +797,8 @@
     in_line = lax.axis_size("row") == 4 and lax.axis_size("col") == 2
     in_line = in_line and lax.axis_size("layer") == 4
     if in_line and fits_line(amplitudes, integrals):
-        ladder = line_exchange(amplitudes, integrals)
-    else:
-        ladder = gathered(amplitudes, integrals)
+        return line_exchange(amplitudes, integrals, occ_energy, vir_energy)
+    ladder = gathered(amplitudes, integrals)
     pair_rows = ladder.shape[0]
     slab_cols = ladder.shape[1]
     occupied = occ_energy.shape[0]

time: 357 us -> 344 us (0.964)
  Pallas kernels: 336 us -> 330 us
  other arithmetic: 4.36 us -> 0 us
    unnamed x3 -> x1, local copies, waits for them, and re-layouts: 1.23 us -> 8.86 us
    pallas_call x1, Pallas kernels: 336 us -> 330 us  [line_exchange(): pl.pallas_call(functools.partial(line_kernel, near), out_shape=(block, bl...]
    pad x2 -> x0, local copies, waits for them, and re-layouts: 4.38 us -> none  [the longest x1 3.46 us: line_exchange(): columns = jnp.pad(integrals, ((0, chunks * CHUNK - depth), (0, 0)))]
where the time goes in v2:
time: 344 us; the launch traced here: 343 us
  Pallas kernels  330 us (96%)
  local copies, waits for them, and re-layouts  12.1 us (4%)
    pallas_call x1, Pallas kernels, line_exchange(): pl.pallas_call(functools.partial(line_kernel, near), out_shape=(block, bl...  330 us
    unnamed x1, local copies, waits for them, and re-layouts  8.86 us

profile of v2, /device:TPU:4, one launch (start us, length us, event | category | flops | bytes accessed | tf_op | source)
XLA Modules:
  0.0 343.0 jit_solution(17102707813682121433)
XLA Ops:
  0.6 8.9 %copy.7.v_hbm = f32[9192,192]{1,0:T(8,128)} copy(f32[9192,192]{0,1:T(8,128)} %param.5) | data formatting | bytes 14118912 | tf_op args[1]
  9.5 330.3 %shard_map.59 = (f32[2,48,512]{2,1,0:T(8,128)}, f32[2,48,512]{2,1,0:T(8,128)}) custom-call(f32[504,9192]{1,0:T(8,128)} %t_hbm.1, f32[9192,192]{1,0:T(8,128)} %copy.7.v_hbm, f32[64]{0:T(128)} %occ_hbm.1, f32[384]{0:T(512)} %vir_hbm.1), custom_call_target="tpu_custom_call" | custom-call | flops 26684743680 | bytes 25590528 | tf_op jit(solution)/shard_map/pallas_call | solution.py:727
  339.8 1.0 slice_bitcast_fusion
  340.8 0.2 copy.9
  341.0 0.9 reshape.11
  341.9 0.2 copy.8
  342.1 0.9 reshape.10

commit v3 on v2

--- a/solution.py
+++ b/solution.py
@@ -12,7 +12,6 @@
 CHUNK = 384
 PIECE = 16
 LAG = 4
-STAGES = 4
 
 
 def lookup(indices, values_table):
@@ -109,13 +108,12 @@
     from_y,
     owned,
     relay,
-    stage,
     below,
-    tail,
+    row_tail,
+    column_tail,
     occ,
     vir,
     load_sem,
-    stage_sem,
     whole_sem,
     third_sem,
     lent_sem,
@@ -129,9 +127,8 @@
     pair_rows, depth = t_hbm.shape
     chunks = land.shape[1]
     far = chunks - near
-    thirds = acc.shape[1]
-    group_rows = acc.shape[2]
-    half_rows = group_rows // 2
+    slab = acc.shape[3]
+    thirds = slab // PIECE
     row = lax.axis_index("row")
     col = lax.axis_index("col")
     layer = lax.axis_index("layer")
@@ -162,35 +159,26 @@
         pltpu.make_async_copy(target, target, sem).wait()
 
     def third_rows(third):
-        return pl.ds(pl.multiple_of(third * group_rows, group_rows), group_rows)
+        return pl.ds(pl.multiple_of(third * PIECE, PIECE), PIECE)
+
+    def depth_at(c):
+        return pl.ds(pl.multiple_of(c * CHUNK, CHUNK), CHUNK)
 
     last_start = (chunks - 1) * CHUNK
     last_depth = depth - last_start
     rows_real = pl.ds(0, pair_rows)
     spare = pl.ds(pair_rows, rows.shape[1] - pair_rows)
 
-    def chunk_at(j):
-        return jnp.where(j < far - 1, near + j, j - (far - 1))
-
-    def stage_copy(j):
-        start = pl.multiple_of(chunk_at(j) * CHUNK, CHUNK)
-        slot = j % STAGES
-        return pltpu.make_async_copy(
-            v_hbm.at[pl.ds(start, CHUNK)], stage.at[slot], stage_sem.at[slot]
-        )
-
-    last_stage = pltpu.make_async_copy(
-        v_hbm.at[pl.ds(last_start, last_depth)],
-        stage.at[STAGES, pl.ds(0, last_depth)],
-        stage_sem.at[STAGES],
+    tails = (
+        pltpu.make_async_copy(
+            v_hbm.at[:, :, :, pl.ds(last_start, last_depth)], column_tail, load_sem.at[0]
+        ),
+        pltpu.make_async_copy(
+            t_hbm.at[:, pl.ds(last_start, last_depth)], row_tail, load_sem.at[1]
+        ),
+        pltpu.make_async_copy(occ_hbm, occ, load_sem.at[2]),
+        pltpu.make_async_copy(vir_hbm, vir, load_sem.at[3]),
     )
-
-    def load_rows(c):
-        start = pl.multiple_of(c * CHUNK, CHUNK)
-        pltpu.make_async_copy(
-            t_hbm.at[:, pl.ds(start, CHUNK)], rows.at[c, rows_real], load_sem.at[0]
-        ).start()
-
     barrier = pltpu.get_barrier_semaphore()
     owned[...] = jnp.zeros_like(owned)
     for step in range(1, 4):
@@ -199,120 +187,84 @@
         )
     for mate in (core_mate, x_mate, y_mate):
         pl.semaphore_signal(barrier, inc=1, device_id=mate, device_id_type=MESH)
-    for j in range(STAGES):
-        stage_copy(j).start()
-    if last_depth < CHUNK:
-        lost = pl.ds(last_depth, CHUNK - last_depth)
-        stage[STAGES, lost] = jnp.zeros_like(stage[STAGES, lost])
-        rows[chunks - 1] = jnp.zeros_like(rows[chunks - 1])
-    last_stage.start()
-    last_rows = (
-        t_hbm.at[:, pl.ds(last_start, last_depth)],
-        tail,
-        load_sem.at[1],
-    )
-    slab = thirds * PIECE
-
-    def turn(slot, c):
-        turned = stage[slot].T
-        for third in range(thirds):
-            for at_core in range(2):
-                for at_x in range(2):
-                    source = (at_x * 2 + at_core) * slab + third * PIECE
-                    target = third * group_rows + at_core * half_rows + at_x * PIECE
-                    land[0, c, pl.ds(target, PIECE)] = turned[source : source + PIECE]
-
-    def prepare(j):
-        c = chunk_at(j)
-        stage_copy(j).wait()
-        turn(j % STAGES, c)
-
-        @pl.when(j + STAGES < chunks - 1)
-        def _():
-            stage_copy(j + STAGES).start()
-
-        load_rows(c)
-
-    def send_far(c):
+    for copy in tails:
+        copy.start()
+    land[0, chunks - 1] = jnp.zeros_like(land[0, chunks - 1])
+    tails[0].wait()
+    land[0, chunks - 1, :, :, :, pl.ds(0, last_depth)] = column_tail[...]
+
+    def send_far(source, c):
         @pl.when(edge)
         def _():
             remote(
-                land.at[0, c], land.at[1, c], sent_sem.at[0], whole_sem.at[1, c],
+                source, land.at[1, c], sent_sem.at[0], whole_sem.at[1, c],
                 {"row": inner_row},
             ).start()
 
         @pl.when(jnp.logical_not(edge))
         def _():
             remote(
-                land.at[0, c], land.at[2, c], sent_sem.at[0], whole_sem.at[2, c],
+                source, land.at[2, c], sent_sem.at[0], whole_sem.at[2, c],
                 {"row": far_inner},
             ).start()
             remote(
-                land.at[0, c], land.at[1, c], sent_sem.at[1], whole_sem.at[1, c],
+                source, land.at[1, c], sent_sem.at[1], whole_sem.at[1, c],
                 {"row": edge_row},
             ).start()
 
-    def send_near(c):
-        remote(
-            land.at[0, c], land.at[2, c], sent_sem.at[2], whole_sem.at[2, c],
-            {"row": far_inner},
-        ).start()
-
-    prepare(0)
     pl.semaphore_wait(barrier, 6)
 
-    def far_loop(j, carry):
-        prepare(j)
-        send_far(near + j - 1)
+    def far_loop(c, carry):
+        send_far(v_hbm.at[:, :, :, depth_at(c)], c)
         return carry
 
-    lax.fori_loop(1, far - 1, far_loop, 0)
-    last_stage.wait()
-    turn(STAGES, chunks - 1)
-    send_far(chunks - 2)
-    pltpu.make_async_copy(*last_rows).start()
-    prepare(far - 1)
-    send_far(chunks - 1)
+    lax.fori_loop(near, chunks - 1, far_loop, 0)
+    send_far(land.at[0, chunks - 1], chunks - 1)
 
     @pl.when(edge)
     def _():
         def send_lent(c, carry):
-            start = pl.multiple_of(c * CHUNK, CHUNK)
-            remote(
-                t_hbm.at[:, pl.ds(start, CHUNK)], lent.at[c, rows_real], sent_sem.at[1],
+            remote(
+                t_hbm.at[:, depth_at(c)], lent.at[c, rows_real], sent_sem.at[1],
                 lent_sem.at[c], {"row": inner_row},
             ).start()
             return carry
 
-        lax.fori_loop(0, near, send_lent, 0)
-
-    def near_loop(c, carry):
-        prepare(far - 1 + c)
-        pl.when(jnp.logical_not(edge))(lambda: send_near(c - 1))
-        return carry
-
-    lax.fori_loop(1, near, near_loop, 0)
-    acc[...] = jnp.zeros_like(acc)
-
-    @pl.when(edge)
-    def _():
         def send_piece(n, carry):
             third, c = n // near, n % near
             remote(
-                land.at[0, c, third_rows(third)], land.at[1, c, third_rows(third)],
+                v_hbm.at[:, :, third_rows(third), depth_at(c)],
+                land.at[1, c, :, :, third_rows(third)],
                 sent_sem.at[2], third_sem.at[0, n], {"row": inner_row},
             ).start()
             return carry
 
+        lax.fori_loop(0, near, send_lent, 0)
         lax.fori_loop(0, near * thirds, send_piece, 0)
 
-    pl.when(jnp.logical_not(edge))(lambda: send_near(near - 1))
-    energies = (
-        pltpu.make_async_copy(occ_hbm, occ, load_sem.at[2]),
-        pltpu.make_async_copy(vir_hbm, vir, load_sem.at[3]),
-    )
-    for copy in energies:
-        copy.start()
+    @pl.when(jnp.logical_not(edge))
+    def _():
+        def send_near(c, carry):
+            remote(
+                v_hbm.at[:, :, :, depth_at(c)], land.at[2, c], sent_sem.at[2],
+                whole_sem.at[2, c], {"row": far_inner},
+            ).start()
+            return carry
+
+        lax.fori_loop(0, near, send_near, 0)
+
+    def load_chunk(c, carry):
+        pltpu.make_async_copy(
+            t_hbm.at[:, depth_at(c)], rows.at[c, rows_real], load_sem.at[4]
+        ).start()
+        pltpu.make_async_copy(
+            v_hbm.at[:, :, :, depth_at(c)], land.at[0, c], load_sem.at[5]
+        ).start()
+        return carry
+
+    lax.fori_loop(0, chunks - 1, load_chunk, 0)
+    acc[...] = jnp.zeros_like(acc)
+    rows[chunks - 1] = jnp.zeros_like(rows[chunks - 1])
 
     def clear_rows(c, carry):
         rows[c, spare] = jnp.zeros_like(rows[c, spare])
@@ -324,28 +276,27 @@
 
     lax.fori_loop(0, chunks - 1, clear_rows, 0)
     lax.fori_loop(0, near, clear_lent, 0)
-    for copy in energies:
+    for copy in tails[1:]:
         copy.wait()
+    rows[chunks - 1, rows_real, pl.ds(0, last_depth)] = row_tail[...]
     denominators(pair_rows, occ, vir, below)
-    arrived(rows.at[pl.ds(0, chunks - 1), rows_real], load_sem.at[0])
-    pltpu.make_async_copy(*last_rows).wait()
-    rows[chunks - 1, rows_real, pl.ds(0, last_depth)] = tail[...]
+    loaded = pl.ds(0, chunks - 1)
+    arrived(rows.at[loaded, rows_real], load_sem.at[4])
+    arrived(land.at[0, loaded], load_sem.at[5])
 
     def add_whole(block, c, pairs):
         other = split(block[c])
         for slot, part in pairs:
-            sums = product(split(land[part, c]), other)
-            acc[slot] += sums.reshape(acc.shape[1:])
+            columns = land[part, c].reshape(-1, CHUNK)
+            acc[slot] += product(split(columns), other).reshape(acc.shape[1:])
 
     def add_third(block, c, third, pairs):
         other = split(block[c])
         for slot, part in pairs:
-            acc[slot, third] += product(split(land[part, c, third_rows(third)]), other)
-
-    half_mine = pl.ds(pl.multiple_of(core * half_rows, half_rows), half_rows)
-    half_given = pl.ds(pl.multiple_of((1 - core) * half_rows, half_rows), half_rows)
-    mine = pl.ds(pl.multiple_of(core * half_rows + x_side * PIECE, PIECE), PIECE)
-    x_given = pl.ds(pl.multiple_of(core * half_rows + (1 - x_side) * PIECE, PIECE), PIECE)
+            at = third_rows(third)
+            columns = land[part, c, :, :, at].reshape(-1, CHUNK)
+            sums = product(split(columns), other)
+            acc[slot, :, :, at] += sums.reshape(2, 2, PIECE, -1)
 
     class Unit:
         def __init__(self, index, slots, group, here, there):
@@ -363,21 +314,21 @@
 
         def core_copy(self):
             return remote(
-                acc.at[self.slots, self.group, half_given],
-                from_core.at[self.slots, self.group],
+                acc.at[self.slots, :, 1 - core, self.group],
+                from_core.at[self.slots, :, self.group],
                 hop_send.at[self.index, 0], hop_recv.at[self.index, 0], core_mate,
             )
 
         def x_copy(self):
             return remote(
-                acc.at[self.slots, self.group, x_given],
+                acc.at[self.slots, 1 - x_side, core, self.group],
                 from_x.at[self.slots, self.group],
                 hop_send.at[self.index, 1], hop_recv.at[self.index, 1], x_mate,
             )
 
         def y_copy(self):
             return remote(
-                acc.at[self.given, self.group, mine],
+                acc.at[self.given, x_side, core, self.group],
                 from_y.at[self.given, self.group],
                 hop_send.at[self.index, 2], hop_recv.at[self.index, 2], y_mate,
             )
@@ -387,12 +338,13 @@
 
         def second(self):
             self.core_copy().wait()
-            acc[self.slots, self.group, half_mine] += from_core[self.slots, self.group]
+            at = (self.slots, slice(None), core, self.group)
+            acc[at] += from_core[self.slots, :, self.group]
             self.x_copy().start()
 
         def third(self):
             self.x_copy().wait()
-            acc[self.slots, self.group, mine] += from_x[self.slots, self.group]
+            acc[self.slots, x_side, core, self.group] += from_x[self.slots, self.group]
             when(self.gives, lambda: self.y_copy().start())
 
         def last(self, targets_here, targets_there=()):
@@ -400,13 +352,14 @@
 
             def take():
                 self.y_copy().wait_recv()
-                acc[self.kept, self.group, mine] += from_y[self.kept, self.group]
+                at = (self.kept, x_side, core, self.group)
+                acc[at] += from_y[self.kept, self.group]
 
             when(self.takes, take)
 
             def deliver(targets):
                 for slot, target, device, send, recv in targets:
-                    source = acc.at[slot, self.group, mine]
+                    source = acc.at[slot, x_side, core, self.group]
                     if device is None:
                         target[self.group] = source[...]
                     else:
@@ -432,7 +385,7 @@
         else:
             pl.when(condition)(action)
 
-    every = pl.ds(0, thirds)
+    every = pl.ds(0, slab)
 
     def kind_sem(kind, group):
         return home_recv.at[kind * thirds + group]
@@ -468,7 +421,7 @@
 
         def sent_home(send, group):
             remote(
-                acc.at[0, group, mine], owned.at[0, group],
+                acc.at[0, x_side, core, group], owned.at[0, group],
                 home_send.at[send], home_recv.at[0], {"row": inner_row},
             ).wait_send()
 
@@ -560,13 +513,13 @@
         )
 
         def edge_unit(third):
-            return Unit(2 + third, pl.ds(4, 1), third, 4, None)
+            return Unit(2 + third, pl.ds(4, 1), third_rows(third), 4, None)
 
         def edge_targets(third):
             return ((4, owned.at[1], edge_row, 2 + third, kind_sem(1, third)),)
 
         def last_unit(third):
-            return Unit(2 + thirds + third, pl.ds(5, 2), third, 5, None)
+            return Unit(2 + thirds + third, pl.ds(5, 2), third_rows(third), 5, None)
 
         def last_targets(third):
             return (
@@ -578,9 +531,10 @@
 
         def pass_on(n):
             third, c = n // near, n % near
-            arrived(land.at[1, c, third_rows(third)], third_sem.at[0, n])
-            remote(
-                land.at[1, c, third_rows(third)], land.at[3, c, third_rows(third)],
+            at = third_rows(third)
+            arrived(land.at[1, c, :, :, at], third_sem.at[0, n])
+            remote(
+                land.at[1, c, :, :, at], land.at[3, c, :, :, at],
                 sent_sem.at[6], third_sem.at[1, n], {"row": far_inner},
             ).start()
             add_third(rows, c, third, ((4, 1),))
@@ -592,7 +546,7 @@
             def _():
                 pass_on(n + LAG)
 
-            arrived(land.at[3, c, third_rows(third)], third_sem.at[1, n])
+            arrived(land.at[3, c, :, :, third_rows(third)], third_sem.at[1, n])
             add_third(rows, c, third, ((5, 3),))
             add_third(lent, c, third, ((6, 3),))
 
@@ -645,14 +599,14 @@
 
         def sent_home(send, group):
             remote(
-                acc.at[0, group, mine], owned.at[1, group],
+                acc.at[0, x_side, core, group], owned.at[1, group],
                 home_send.at[send], home_recv.at[0], {"row": far_inner},
             ).wait_send()
 
         @pl.when(home)
         def _():
             for send in range(2, 2 + 3 * thirds):
-                sent_home(send, 0)
+                sent_home(send, third_rows(0))
             for kind in range(3):
                 send_relay(kind).wait_send()
 
@@ -681,7 +635,7 @@
 
     def owned_thirds(kind):
         for third in range(thirds):
-            arrived(owned.at[kind, third], kind_sem(kind, third))
+            arrived(owned.at[kind, third_rows(third)], kind_sem(kind, third))
 
     @pl.when(edge & home)
     def _():
@@ -703,10 +657,15 @@
         owned_whole(1)
         owned_whole(2)
 
-    for block, value in ((col, owned[0] + owned[2]), (1 - col, owned[1])):
-        ladder = value.reshape(out.shape[1:])
-        out[block] = ladder
-        step_out[block] = ladder / below[block]
+    edge_sum = owned[0] + owned[2]
+    inner_sum = owned[1]
+    real = slice(0, pair_rows)
+    for block, own_col in ((0, col == 0), (1, col == 1)):
+        ladder = jnp.where(own_col, edge_sum, inner_sum)
+        step = ladder / below[block]
+        lanes = pl.ds(block * pair_rows, pair_rows)
+        out[:, lanes] = ladder[:, real]
+        step_out[:, lanes] = step[:, real]
 
 
 def line_exchange(amplitudes, integrals, occ_energy, vir_energy):
@@ -718,12 +677,13 @@
     slab = width // layers
     thirds = slab // PIECE
     padded = -(-pair_rows // 128) * 128
-    group = width // thirds
+    last_depth = depth - (chunks - 1) * CHUNK
     vmem = functools.partial(pltpu.VMEM, dtype=jnp.float32)
     smem = functools.partial(pltpu.SMEM, dtype=jnp.float32)
     dma = pltpu.SemaphoreType.DMA
     flops = 2 * 3 * 5 * pair_rows * depth * width
-    block = jax.ShapeDtypeStruct((2, slab, padded), jnp.float32)
+    block = jax.ShapeDtypeStruct((slab, 2 * pair_rows), jnp.float32)
+    columns = integrals.T.reshape(layers // 2, 2, slab, depth)
     results = pl.pallas_call(
         functools.partial(line_kernel, near),
         out_shape=(block, block),
@@ -732,20 +692,19 @@
         scratch_shapes=[
             vmem((chunks, padded, CHUNK)),
             vmem((near, padded, CHUNK)),
-            vmem((4, chunks, width, CHUNK)),
-            vmem((7, thirds, group, padded)),
-            vmem((7, thirds, group // 2, padded)),
-            vmem((7, thirds, PIECE, padded)),
-            vmem((7, thirds, PIECE, padded)),
-            vmem((3, thirds, PIECE, padded)),
-            vmem((3, thirds, PIECE, padded)),
-            vmem((STAGES + 1, CHUNK, width)),
+            vmem((4, chunks, 2, 2, slab, CHUNK)),
+            vmem((7, 2, 2, slab, padded)),
+            vmem((7, 2, slab, padded)),
+            vmem((7, slab, padded)),
+            vmem((7, slab, padded)),
+            vmem((3, slab, padded)),
+            vmem((3, slab, padded)),
             vmem((2, slab, padded)),
-            vmem((pair_rows, depth - (chunks - 1) * CHUNK)),
+            vmem((pair_rows, last_depth)),
+            vmem((2, 2, slab, last_depth)),
             smem(occ_energy.shape),
             smem(vir_energy.shape),
-            dma((4,)),
-            dma((STAGES + 1,)),
+            dma((6,)),
             dma((4, chunks)),
             dma((2, near * thirds)),
             dma((near,)),
@@ -762,12 +721,8 @@
         cost_estimate=pl.CostEstimate(
             flops=flops, bytes_accessed=4 * depth * (pair_rows + width), transcendentals=0
         ),
-    )(amplitudes, integrals, occ_energy, vir_energy)
-
-    def placed(value):
-        return value[:, :, :pair_rows].transpose(0, 2, 1).reshape(2 * pair_rows, slab)
-
-    return tuple(placed(value) for value in results)
+    )(amplitudes, columns, occ_energy, vir_energy)
+    return tuple(value.T for value in results)
 
 
 def gathered(amplitudes, integrals):

time: 344 us -> 335 us (0.974)
  local copies, waits for them, and re-layouts: 12.1 us -> 3.23 us
    unnamed x1 -> x2, local copies, waits for them, and re-layouts: 8.86 us -> 3.23 us
where the time goes in v3:
time: 335 us; the launch traced here: 334 us
  Pallas kernels  330 us (99%)
    pallas_call x1, Pallas kernels, line_exchange(): pl.pallas_call(functools.partial(line_kernel, near), out_shape=(block, bl...  330 us

profile of v3, /device:TPU:4, one launch (start us, length us, event | category | flops | bytes accessed | tf_op | source)
XLA Modules:
  0.0 334.2 jit_solution(16689952182495072396)
XLA Ops:
  0.6 330.3 %shard_map.59 = (f32[48,1008]{1,0:T(8,128)}, f32[48,1008]{1,0:T(8,128)}) custom-call(f32[504,9192]{1,0:T(8,128)} %t_hbm.1, f32[2,2,48,9192]{3,2,1,0:T(8,128)} %bitcast.7, f32[64]{0:T(128)} %occ_hbm.1, f32[384]{0:T(512)} %vir_hbm.1), custom_call_target="tpu_custom_call" | custom-call | flops 26684743680 | bytes 25590528 | tf_op jit(solution)/shard_map/pallas_call | solution.py:687
  331.0 1.6 copy.8
  332.6 1.6 copy.9

commit v4 on v3

--- a/solution.py
+++ b/solution.py
@@ -9,9 +9,8 @@
 from jax.sharding import PartitionSpec as P
 
 MESH = pl.DeviceIdType.MESH
-CHUNK = 384
-PIECE = 16
-LAG = 4
+CHUNK = 256
+LAG = 8
 
 
 def lookup(indices, values_table):
@@ -27,6 +26,14 @@
     slab_cols = partial_sum.shape[1] // layer_count
     blocks = partial_sum.reshape(col_count, pair_rows, layer_count, slab_cols)
     return blocks.transpose(0, 2, 1, 3).reshape(col_count * layer_count * pair_rows, slab_cols)
+
+
+def near_chunks(chunks):
+    return -(-5 * chunks // 14)
+
+
+def groups_of(slab):
+    return ((0, slab - 24), (slab - 24, 16), (slab - 8, 8))
 
 
 def split(value):
@@ -98,7 +105,6 @@
     occ_hbm,
     vir_hbm,
     out,
-    step_out,
     rows,
     lent,
     land,
@@ -123,12 +129,14 @@
     home_send,
     home_recv,
     relay_recv,
+    go_sem,
 ):
     pair_rows, depth = t_hbm.shape
     chunks = land.shape[1]
     far = chunks - near
     slab = acc.shape[3]
-    thirds = slab // PIECE
+    groups = groups_of(slab)
+    thirds = len(groups)
     row = lax.axis_index("row")
     col = lax.axis_index("col")
     layer = lax.axis_index("layer")
@@ -159,7 +167,7 @@
         pltpu.make_async_copy(target, target, sem).wait()
 
     def third_rows(third):
-        return pl.ds(pl.multiple_of(third * PIECE, PIECE), PIECE)
+        return pl.ds(*groups[third])
 
     def depth_at(c):
         return pl.ds(pl.multiple_of(c * CHUNK, CHUNK), CHUNK)
@@ -197,18 +205,18 @@
         @pl.when(edge)
         def _():
             remote(
-                source, land.at[1, c], sent_sem.at[0], whole_sem.at[1, c],
+                source, land.at[1, c], sent_sem.at[0], whole_sem.at[c - near],
                 {"row": inner_row},
             ).start()
 
         @pl.when(jnp.logical_not(edge))
         def _():
             remote(
-                source, land.at[2, c], sent_sem.at[0], whole_sem.at[2, c],
+                source, land.at[2, c], sent_sem.at[0], whole_sem.at[far + c],
                 {"row": far_inner},
             ).start()
             remote(
-                source, land.at[1, c], sent_sem.at[1], whole_sem.at[1, c],
+                source, land.at[1, c], sent_sem.at[1], whole_sem.at[c - near],
                 {"row": edge_row},
             ).start()
 
@@ -230,24 +238,24 @@
             ).start()
             return carry
 
-        def send_piece(n, carry):
-            third, c = n // near, n % near
+        def send_piece(third, c, carry):
             remote(
                 v_hbm.at[:, :, third_rows(third), depth_at(c)],
                 land.at[1, c, :, :, third_rows(third)],
-                sent_sem.at[2], third_sem.at[0, n], {"row": inner_row},
+                sent_sem.at[2], third_sem.at[0, third * near + c], {"row": inner_row},
             ).start()
             return carry
 
         lax.fori_loop(0, near, send_lent, 0)
-        lax.fori_loop(0, near * thirds, send_piece, 0)
+        for third in range(thirds):
+            lax.fori_loop(0, near, functools.partial(send_piece, third), 0)
 
     @pl.when(jnp.logical_not(edge))
     def _():
         def send_near(c, carry):
             remote(
                 v_hbm.at[:, :, :, depth_at(c)], land.at[2, c], sent_sem.at[2],
-                whole_sem.at[2, c], {"row": far_inner},
+                whole_sem.at[far + c], {"row": far_inner},
             ).start()
             return carry
 
@@ -296,7 +304,7 @@
             at = third_rows(third)
             columns = land[part, c, :, :, at].reshape(-1, CHUNK)
             sums = product(split(columns), other)
-            acc[slot, :, :, at] += sums.reshape(2, 2, PIECE, -1)
+            acc[slot, :, :, at] += sums.reshape(2, 2, at.size, -1)
 
     class Unit:
         def __init__(self, index, slots, group, here, there):
@@ -357,7 +365,10 @@
 
             when(self.takes, take)
 
-            def deliver(targets):
+            self.deliver(targets_here, targets_there)
+
+        def deliver(self, targets_here, targets_there=()):
+            def go(targets):
                 for slot, target, device, send, recv in targets:
                     source = acc.at[slot, x_side, core, self.group]
                     if device is None:
@@ -369,9 +380,9 @@
                         ).start()
 
             if targets_here:
-                pl.when(home)(lambda: deliver(targets_here))
+                pl.when(home)(lambda: go(targets_here))
             if targets_there:
-                pl.when(jnp.logical_not(home))(lambda: deliver(targets_there))
+                pl.when(jnp.logical_not(home))(lambda: go(targets_there))
 
         def run(self, targets_here, targets_there=()):
             self.start()
@@ -387,6 +398,26 @@
 
     every = pl.ds(0, slab)
 
+    def owned_whole(kind):
+        arrived(owned.at[kind, every], kind_sem(kind, 0))
+
+    def owned_third(kind, third):
+        arrived(owned.at[kind, third_rows(third)], kind_sem(kind, third))
+
+    def put(block, at, value):
+        lanes = pl.ds(block * pair_rows, pair_rows)
+        real = slice(0, pair_rows)
+        out[0, at, lanes] = value[:, real]
+        out[1, at, lanes] = (value / below[block, at])[:, real]
+
+    def put_edge(at):
+        for block in range(2):
+            pl.when(col == block)(lambda: put(block, at, owned[0, at] + owned[2, at]))
+
+    def put_inner(at):
+        for block in range(2):
+            pl.when(col != block)(lambda: put(block, at, owned[1, at]))
+
     def kind_sem(kind, group):
         return home_recv.at[kind * thirds + group]
 
@@ -398,7 +429,8 @@
 
         def other(part, i, carry):
             c = near + i
-            arrived(land.at[part, c], whole_sem.at[part, c])
+            first = (0, far + near, far + chunks)[part - 1]
+            arrived(land.at[part, c], whole_sem.at[first + i])
             add_whole(rows, c, ((part, part),))
             return carry
 
@@ -411,12 +443,14 @@
             )
         )
         lax.fori_loop(0, far, functools.partial(other, 2), 0)
-        Unit(1, pl.ds(2, 1), every, None, 2).run(
-            (), ((2, relay.at[0], far_inner, 1, relay_recv.at[0]),)
-        )
+        second_unit = Unit(1, pl.ds(2, 1), every, None, 2)
+        second_unit.run(())
         lax.fori_loop(0, far, functools.partial(other, 3), 0)
-        Unit(2, pl.ds(3, 1), every, 3, None).run(
-            ((3, owned.at[0], far_edge, 2, kind_sem(0, 0)),)
+        Unit(2, pl.ds(3, 1), every, 3, None).run(())
+        pl.semaphore_wait(go_sem, 1)
+        second_unit.deliver(
+            ((3, owned.at[0], far_edge, 2, kind_sem(0, 0)),),
+            ((2, relay.at[0], far_inner, 1, relay_recv.at[0]),),
         )
 
         def sent_home(send, group):
@@ -439,32 +473,32 @@
             (0, land.at[0, arrived_far]), (2, land.at[0, pl.ds(0, near)]),
         ):
             remote(
-                source, source, sent_sem.at[at], whole_sem.at[0, 0], {"row": inner_row}
+                source, source, sent_sem.at[at], whole_sem.at[0], {"row": inner_row}
             ).wait_send()
         remote(
             rows.at[pl.ds(0, near), rows_real], rows.at[pl.ds(0, near), rows_real],
-            sent_sem.at[1], whole_sem.at[0, 0], {"row": inner_row},
+            sent_sem.at[1], whole_sem.at[0], {"row": inner_row},
         ).wait_send()
 
     @pl.when(jnp.logical_not(edge))
     def _():
         def first_far(i, carry):
             c = near + i
-            arrived(land.at[1, c], whole_sem.at[1, c])
-            remote(
-                land.at[1, c], land.at[3, c], sent_sem.at[3], whole_sem.at[3, c],
+            arrived(land.at[1, c], whole_sem.at[c - near])
+            remote(
+                land.at[1, c], land.at[3, c], sent_sem.at[3], whole_sem.at[far + chunks + c - near],
                 {"row": far_inner},
             ).start()
-            arrived(land.at[2, c], whole_sem.at[2, c])
-            remote(
-                land.at[2, c], land.at[2, c], sent_sem.at[4], whole_sem.at[2, c],
+            arrived(land.at[2, c], whole_sem.at[far + c])
+            remote(
+                land.at[2, c], land.at[2, c], sent_sem.at[4], whole_sem.at[far + c],
                 {"row": edge_row},
             ).start()
             add_whole(rows, c, ((0, 0), (4, 1), (1, 2)))
             return carry
 
         def first_near(c, carry):
-            arrived(land.at[2, c], whole_sem.at[2, c])
+            arrived(land.at[2, c], whole_sem.at[far + c])
             add_whole(rows, c, ((0, 0), (1, 2)))
             return carry
 
@@ -473,44 +507,42 @@
             add_whole(lent, c, ((2, 0), (3, 2)))
             return carry
 
-        def second_far(i, carry):
-            c = near + i
-            arrived(land.at[3, c], whole_sem.at[3, c])
-            remote(
-                land.at[3, c], land.at[3, c], sent_sem.at[5], whole_sem.at[3, c],
+        def second_far(c, carry):
+            arrived(land.at[3, c], whole_sem.at[far + chunks + c - near])
+            remote(
+                land.at[3, c], land.at[3, c], sent_sem.at[5], whole_sem.at[far + chunks + c - near],
                 {"row": edge_row},
             ).start()
             add_whole(rows, c, ((5, 3),))
             return carry
 
         lax.fori_loop(0, far, first_far, 0)
-        early = near // 3
-
-        def early_block(m, carry):
-            lax.fori_loop(3 * m, 3 * m + 3, first_near, 0)
-            return lent_chunk(m, carry)
-
-        lax.fori_loop(0, early, early_block, 0)
-        Unit(0, pl.ds(0, 2), every, 0, 1).run(
-            ((0, owned.at[1], None, 0, None),),
-            ((1, relay.at[1], far_inner, 0, relay_recv.at[1]),),
-        )
-        late = near - early
-        per = far // (late - 1)
-
-        def late_block(m, carry):
-            lax.fori_loop(per * m, per * m + per, second_far, 0)
-            return lent_chunk(early + m, carry)
-
-        lax.fori_loop(0, late - 1, late_block, 0)
-        lax.fori_loop(per * (late - 1), far, second_far, 0)
-        lent_chunk(near - 1, 0)
+
+        def lent_due(step):
+            due = (8 * step - 1) // 21
+            return jnp.where(step < 1, 0, jnp.minimum(due, near))
+
+        def with_lent(body, step, carry):
+            body(step, carry)
+            count = lent_due(step)
+
+            @pl.when(count > lent_due(step - 1))
+            def _():
+                lent_chunk(count - 1, 0)
+
+            return carry
+
+        lax.fori_loop(0, near, functools.partial(with_lent, first_near), 0)
+        own_unit = Unit(0, pl.ds(0, 2), every, 0, 1)
+        own_unit.run(((0, owned.at[1], None, 0, None),))
+        lax.fori_loop(near, chunks, functools.partial(with_lent, second_far), 0)
+        left = near - (8 * (chunks - 1) - 1) // 21
+        for j in range(max(left, 0)):
+            lent_chunk(near - left + j, 0)
 
         lent_unit = Unit(1, pl.ds(2, 2), every, 2, 3)
-        lent_targets = (
-            ((2, owned.at[2], None, 0, None),),
-            ((3, relay.at[2], far_inner, 1, relay_recv.at[2]),),
-        )
+        own_targets = ((1, relay.at[1], far_inner, 0, relay_recv.at[1]),)
+        lent_targets = ((3, relay.at[2], far_inner, 1, relay_recv.at[2]),)
 
         def edge_unit(third):
             return Unit(2 + third, pl.ds(4, 1), third_rows(third), 4, None)
@@ -527,10 +559,8 @@
                 (6, owned.at[2], far_edge, 2 + 2 * thirds + third, kind_sem(2, third)),
             )
 
-        pieces = near * thirds
-
-        def pass_on(n):
-            third, c = n // near, n % near
+        def pass_on(third, c):
+            n = third * near + c
             at = third_rows(third)
             arrived(land.at[1, c, :, :, at], third_sem.at[0, n])
             remote(
@@ -539,37 +569,48 @@
             ).start()
             add_third(rows, c, third, ((4, 1),))
 
-        def near_step(n, carry):
-            third, c = n // near, n % near
-
-            @pl.when(n + LAG < pieces)
-            def _():
-                pass_on(n + LAG)
-
-            arrived(land.at[3, c, :, :, third_rows(third)], third_sem.at[1, n])
+        def near_step(third, c, carry):
+            ahead = c + LAG
+            pl.when(ahead < near)(lambda: pass_on(third, ahead))
+            if third + 1 < thirds:
+                pl.when(ahead >= near)(lambda: pass_on(third + 1, ahead - near))
+            at = third_rows(third)
+            arrived(land.at[3, c, :, :, at], third_sem.at[1, third * near + c])
             add_third(rows, c, third, ((5, 3),))
             add_third(lent, c, third, ((6, 3),))
 
-            first = third == 0
-            later = jnp.logical_not(first)
-            before = third - 1
-            pl.when(first & (c == 1))(lent_unit.start)
-            pl.when(first & (c == 3))(lent_unit.second)
-            pl.when(first & (c == 5))(lent_unit.third)
-            pl.when(first & (c == 7))(lambda: lent_unit.last(*lent_targets))
-            pl.when(later & (c == 1))(lambda: last_unit(before).start())
-            pl.when(later & (c == 3))(lambda: last_unit(before).second())
-            pl.when(later & (c == 5))(lambda: last_unit(before).third())
-            pl.when(later & (c == 7))(
-                lambda: last_unit(before).last(last_targets(before))
+            def stage(step, action):
+                pl.when(c == step)(action)
+
+            if third == 0:
+                stage(0, lent_unit.start)
+                stage(2, lent_unit.second)
+                stage(6, lent_unit.third)
+                stage(10, lambda: lent_unit.last(((2, owned.at[2], None, 0, None),)))
+            else:
+                before = third - 1
+                late = before + 2 == thirds
+                stage(0, last_unit(before).start)
+                stage(2, last_unit(before).second)
+                stage(7, last_unit(before).third)
+                if not late:
+                    stage(near - 1, lambda: last_unit(before).last(()))
+                stage(1, edge_unit(before).third)
+                stage(5, lambda: edge_unit(before).last(edge_targets(before)))
+            stage(near - LAG, edge_unit(third).start)
+            stage(near - LAG + 2, edge_unit(third).second)
+            if third + 1 == thirds:
+                stage(near - LAG, cross)
+            return carry
+
+        def cross():
+            pl.semaphore_signal(
+                go_sem, inc=1, device_id={"row": edge_row}, device_id_type=MESH
             )
-            pl.when(c == near - LAG)(lambda: edge_unit(third).start())
-            pl.when(c == near - LAG + 2)(lambda: edge_unit(third).second())
-            pl.when(later & (c == 0))(lambda: edge_unit(before).third())
-            pl.when(later & (c == 2))(
-                lambda: edge_unit(before).last(edge_targets(before))
-            )
-            return carry
+            own_unit.deliver((), own_targets)
+            lent_unit.deliver((), lent_targets)
+            for third in range(thirds - 2):
+                last_unit(third).deliver(last_targets(third))
 
         def send_relay(kind):
             return remote(
@@ -583,19 +624,28 @@
                 arrived(relay.at[kind], relay_recv.at[kind])
                 send_relay(kind).start()
 
-        for n in range(LAG):
-            pass_on(n)
-        lax.fori_loop(0, pieces, near_step, 0)
+        for c in range(LAG):
+            pass_on(0, c)
+        for third in range(thirds):
+            lax.fori_loop(0, near, functools.partial(near_step, third), 0)
         final = thirds - 1
         last_unit(final).start()
         edge_unit(final).third()
+        last_unit(final - 1).last(last_targets(final - 1))
+        last_unit(final).second()
+
+        @pl.when(home)
+        def _():
+            owned_whole(0)
+            put_edge(every)
+            put_inner(every)
+
         relay_on(1)
-        last_unit(final).second()
         edge_unit(final).last(edge_targets(final))
+        last_unit(final).third()
         relay_on(2)
-        last_unit(final).third()
+        relay_on(0)
         last_unit(final).last(last_targets(final))
-        relay_on(0)
 
         def sent_home(send, group):
             remote(
@@ -605,8 +655,9 @@
 
         @pl.when(home)
         def _():
-            for send in range(2, 2 + 3 * thirds):
-                sent_home(send, third_rows(0))
+            for at in range(3):
+                for third in range(thirds):
+                    sent_home(2 + at * thirds + third, third_rows(third))
             for kind in range(3):
                 send_relay(kind).wait_send()
 
@@ -627,68 +678,55 @@
             (6, land.at[1, arrived_near]),
         ):
             remote(
-                source, source, sent_sem.at[at], whole_sem.at[0, 0], {"row": far_inner}
+                source, source, sent_sem.at[at], whole_sem.at[0], {"row": far_inner}
             ).wait_send()
-
-    def owned_whole(kind):
-        arrived(owned.at[kind, every], kind_sem(kind, 0))
-
-    def owned_thirds(kind):
-        for third in range(thirds):
-            arrived(owned.at[kind, third_rows(third)], kind_sem(kind, third))
 
     @pl.when(edge & home)
     def _():
-        owned_thirds(1)
-
-    @pl.when(jnp.logical_not(edge) & home)
-    def _():
-        owned_whole(0)
+        put_edge(every)
+        for third in range(thirds):
+            owned_third(1, third)
+            put_inner(third_rows(third))
 
     @pl.when(edge & jnp.logical_not(home))
     def _():
         owned_whole(0)
-        owned_thirds(1)
-        owned_thirds(2)
+        for third in range(thirds):
+            owned_third(1, third)
+            put_inner(third_rows(third))
+            owned_third(2, third)
+            put_edge(third_rows(third))
 
     @pl.when(jnp.logical_not(edge) & jnp.logical_not(home))
     def _():
+        owned_whole(1)
+        put_inner(every)
+        owned_whole(2)
         owned_whole(0)
-        owned_whole(1)
-        owned_whole(2)
-
-    edge_sum = owned[0] + owned[2]
-    inner_sum = owned[1]
-    real = slice(0, pair_rows)
-    for block, own_col in ((0, col == 0), (1, col == 1)):
-        ladder = jnp.where(own_col, edge_sum, inner_sum)
-        step = ladder / below[block]
-        lanes = pl.ds(block * pair_rows, pair_rows)
-        out[:, lanes] = ladder[:, real]
-        step_out[:, lanes] = step[:, real]
+        put_edge(every)
 
 
 def line_exchange(amplitudes, integrals, occ_energy, vir_energy):
     pair_rows = amplitudes.shape[0]
     depth, width = integrals.shape
     chunks = -(-depth // CHUNK)
-    near = 3 * chunks // 8
+    near = near_chunks(chunks)
     layers = lax.axis_size("layer")
     slab = width // layers
-    thirds = slab // PIECE
+    groups = groups_of(slab)
+    thirds = len(groups)
     padded = -(-pair_rows // 128) * 128
     last_depth = depth - (chunks - 1) * CHUNK
     vmem = functools.partial(pltpu.VMEM, dtype=jnp.float32)
     smem = functools.partial(pltpu.SMEM, dtype=jnp.float32)
     dma = pltpu.SemaphoreType.DMA
     flops = 2 * 3 * 5 * pair_rows * depth * width
-    block = jax.ShapeDtypeStruct((slab, 2 * pair_rows), jnp.float32)
     columns = integrals.T.reshape(layers // 2, 2, slab, depth)
-    results = pl.pallas_call(
+    result = pl.pallas_call(
         functools.partial(line_kernel, near),
-        out_shape=(block, block),
+        out_shape=jax.ShapeDtypeStruct((2, slab, 2 * pair_rows), jnp.float32),
         in_specs=[pl.BlockSpec(memory_space=pl.ANY)] * 4,
-        out_specs=[pl.BlockSpec(memory_space=pltpu.VMEM)] * 2,
+        out_specs=pl.BlockSpec(memory_space=pltpu.VMEM),
         scratch_shapes=[
             vmem((chunks, padded, CHUNK)),
             vmem((near, padded, CHUNK)),
@@ -705,7 +743,7 @@
             smem(occ_energy.shape),
             smem(vir_energy.shape),
             dma((6,)),
-            dma((4, chunks)),
+            dma((3 * chunks - 2 * near,)),
             dma((2, near * thirds)),
             dma((near,)),
             dma((7,)),
@@ -714,6 +752,7 @@
             dma((5 + 3 * thirds,)),
             dma((3 * thirds,)),
             dma((3,)),
+            pltpu.SemaphoreType.REGULAR,
         ],
         compiler_params=pltpu.CompilerParams(
             collective_id=0, has_side_effects=True, vmem_limit_bytes=67043328
@@ -722,7 +761,7 @@
             flops=flops, bytes_accessed=4 * depth * (pair_rows + width), transcendentals=0
         ),
     )(amplitudes, columns, occ_energy, vir_energy)
-    return tuple(value.T for value in results)
+    return result[0].T, result[1].T
 
 
 def gathered(amplitudes, integrals):
@@ -742,10 +781,10 @@
     pair_rows = amplitudes.shape[0]
     depth, width = integrals.shape
     chunks = -(-depth // CHUNK)
-    near = 3 * chunks // 8
-    split_evenly = width % (4 * PIECE) == 0 and pair_rows % 8 == 0 and near % 3 == 0
+    near = near_chunks(chunks)
+    even = width % 32 == 0 and width >= 128 and pair_rows % 8 == 0
     words = chunks * (4 * width + pair_rows) + near * pair_rows
-    return split_evenly and near >= 9 and words * CHUNK * 4 < 56 * 2**20
+    return even and near >= 13 and words * CHUNK * 4 < 56 * 2**20
 
 
 def shards(amplitudes, integrals, occ_energy, vir_energy):

time: 335 us -> 328 us (0.979)
  Pallas kernels: 330 us -> 326 us
    pallas_call x1, Pallas kernels: 330 us -> 326 us  [line_exchange(): pl.pallas_call(functools.partial(line_kernel, near), out_shape=jax.ShapeD...]
where the time goes in v4:
time: 328 us
  Pallas kernels  326 us (99%)
    pallas_call x1, Pallas kernels, line_exchange(): pl.pallas_call(functools.partial(line_kernel, near), out_shape=jax.ShapeD...  326 us

profile of v4, /device:TPU:4, one launch (start us, length us, event | category | flops | bytes accessed | tf_op | source)
XLA Modules:
  0.0 327.9 jit_solution(5139723782030105500)
XLA Ops:
  0.6 325.5 %shard_map.59 = f32[2,48,1008]{2,1,0:T(8,128)} custom-call(f32[504,9192]{1,0:T(8,128)} %t_hbm.1, f32[2,2,48,9192]{3,2,1,0:T(8,128)} %bitcast.11, f32[64]{0:T(128)} %occ_hbm.1, f32[384]{0:T(512)} %vir_hbm.1), custom_call_target="tpu_custom_call" | custom-call | flops 26684743680 | bytes 25590528 | tf_op jit(solution)/shard_map/pallas_call | solution.py:725
  326.2 1.8 slice_bitcast_fusion

commit v5 on v4

--- a/solution.py
+++ b/solution.py
@@ -112,6 +112,7 @@
     from_core,
     from_x,
     from_y,
+    from_cross,
     owned,
     relay,
     below,
@@ -152,6 +153,7 @@
     core_mate = {"layer": x_side * 2 + (1 - core)}
     x_mate = {"layer": (1 - x_side) * 2 + core}
     y_mate = {"col": 1 - col}
+    cross_mate = {"col": 1 - col, "layer": (1 - x_side) * 2 + core}
 
     def remote(source, target, send_sem, recv_sem, device):
         return pltpu.make_async_remote_copy(
@@ -193,7 +195,7 @@
         pl.semaphore_signal(
             barrier, inc=1, device_id={"row": (row + step) % 4}, device_id_type=MESH
         )
-    for mate in (core_mate, x_mate, y_mate):
+    for mate in (core_mate, x_mate, y_mate, cross_mate):
         pl.semaphore_signal(barrier, inc=1, device_id=mate, device_id_type=MESH)
     for copy in tails:
         copy.start()
@@ -220,7 +222,7 @@
                 {"row": edge_row},
             ).start()
 
-    pl.semaphore_wait(barrier, 6)
+    pl.semaphore_wait(barrier, 7)
 
     def far_loop(c, carry):
         send_far(v_hbm.at[:, :, :, depth_at(c)], c)
@@ -383,6 +385,40 @@
                 pl.when(home)(lambda: go(targets_here))
             if targets_there:
                 pl.when(jnp.logical_not(home))(lambda: go(targets_there))
+
+        def cross_copy(self):
+            return remote(
+                acc.at[self.slots, 1 - x_side, core, self.group], from_cross,
+                hop_send.at[0, 3], hop_recv.at[0, 3], cross_mate,
+            )
+
+        def scatter(self):
+            self.core_copy().wait()
+            at = (self.slots, slice(None), core, self.group)
+            acc[at] += from_core[self.slots, :, self.group]
+            when(home, lambda: self.x_copy().start())
+
+            @pl.when(jnp.logical_not(home))
+            def _():
+                self.cross_copy().start()
+                self.y_copy().start()
+
+        def gather(self, targets):
+            @pl.when(home)
+            def _():
+                self.x_copy().wait()
+                self.y_copy().wait_recv()
+                at = (self.slots, x_side, core, self.group)
+                near_sum = from_x[self.slots, self.group] + from_y[self.slots, self.group]
+                self.cross_copy().wait_recv()
+                acc[at] += near_sum + from_cross[...]
+
+            @pl.when(jnp.logical_not(home))
+            def _():
+                self.y_copy().wait_send()
+                self.cross_copy().wait_send()
+
+            self.deliver(targets)
 
         def run(self, targets_here, targets_there=()):
             self.start()
@@ -632,7 +668,7 @@
         last_unit(final).start()
         edge_unit(final).third()
         last_unit(final - 1).last(last_targets(final - 1))
-        last_unit(final).second()
+        last_unit(final).scatter()
 
         @pl.when(home)
         def _():
@@ -642,10 +678,15 @@
 
         relay_on(1)
         edge_unit(final).last(edge_targets(final))
-        last_unit(final).third()
-        relay_on(2)
-        relay_on(0)
-        last_unit(final).last(last_targets(final))
+
+        @pl.when(home)
+        def _():
+            for kind in (2, 0):
+                arrived(relay.at[kind], relay_recv.at[kind])
+            relay[2] += relay[0]
+            send_relay(2).start()
+
+        last_unit(final).gather(last_targets(final))
 
         def sent_home(send, group):
             remote(
@@ -658,7 +699,7 @@
             for at in range(3):
                 for third in range(thirds):
                     sent_home(2 + at * thirds + third, third_rows(third))
-            for kind in range(3):
+            for kind in (1, 2):
                 send_relay(kind).wait_send()
 
         @pl.when(jnp.logical_not(home))
@@ -702,7 +743,6 @@
         owned_whole(1)
         put_inner(every)
         owned_whole(2)
-        owned_whole(0)
         put_edge(every)
 
 
@@ -735,6 +775,7 @@
             vmem((7, 2, slab, padded)),
             vmem((7, slab, padded)),
             vmem((7, slab, padded)),
+            vmem((2, groups[-1][1], padded)),
             vmem((3, slab, padded)),
             vmem((3, slab, padded)),
             vmem((2, slab, padded)),
@@ -747,8 +788,8 @@
             dma((2, near * thirds)),
             dma((near,)),
             dma((7,)),
-            dma((2 + 2 * thirds, 3)),
-            dma((2 + 2 * thirds, 3)),
+            dma((2 + 2 * thirds, 4)),
+            dma((2 + 2 * thirds, 4)),
             dma((5 + 3 * thirds,)),
             dma((3 * thirds,)),
             dma((3,)),

time: 328 us -> 326 us (level)
  no operation moved by 1% of the time
where the time goes in v5:
time: 326 us
  Pallas kernels  324 us (99%)
    pallas_call x1, Pallas kernels, line_exchange(): pl.pallas_call(functools.partial(line_kernel, near), out_shape=jax.ShapeD...  324 us

profile of v5, /device:TPU:4, one launch (start us, length us, event | category | flops | bytes accessed | tf_op | source)
XLA Modules:
  0.0 326.3 jit_solution(13788627857693085806)
XLA Ops:
  0.6 323.9 %shard_map.59 = f32[2,48,1008]{2,1,0:T(8,128)} custom-call(f32[504,9192]{1,0:T(8,128)} %t_hbm.1, f32[2,2,48,9192]{3,2,1,0:T(8,128)} %bitcast.11, f32[64]{0:T(128)} %occ_hbm.1, f32[384]{0:T(512)} %vir_hbm.1), custom_call_target="tpu_custom_call" | custom-call | flops 26684743680 | bytes 25590528 | tf_op jit(solution)/shard_map/pallas_call | solution.py:765
  324.5 1.8 slice_bitcast_fusion

commit v6 on v5

--- a/solution.py
+++ b/solution.py
@@ -10,7 +10,7 @@
 
 MESH = pl.DeviceIdType.MESH
 CHUNK = 256
-LAG = 8
+LAG = 10
 
 
 def lookup(indices, values_table):
@@ -127,6 +127,7 @@
     sent_sem,
     hop_send,
     hop_recv,
+    cross_sem,
     home_send,
     home_recv,
     relay_recv,
@@ -389,7 +390,7 @@
         def cross_copy(self):
             return remote(
                 acc.at[self.slots, 1 - x_side, core, self.group], from_cross,
-                hop_send.at[0, 3], hop_recv.at[0, 3], cross_mate,
+                cross_sem.at[0], cross_sem.at[1], cross_mate,
             )
 
         def scatter(self):
@@ -788,8 +789,9 @@
             dma((2, near * thirds)),
             dma((near,)),
             dma((7,)),
-            dma((2 + 2 * thirds, 4)),
-            dma((2 + 2 * thirds, 4)),
+            dma((2 + 2 * thirds, 3)),
+            dma((2 + 2 * thirds, 3)),
+            dma((2,)),
             dma((5 + 3 * thirds,)),
             dma((3 * thirds,)),
             dma((3,)),

time: 326 us -> 327 us (level)
  no operation moved by 1% of the time
where the time goes in v6:
time: 327 us
  Pallas kernels  325 us (99%)
    pallas_call x1, Pallas kernels, line_exchange(): pl.pallas_call(functools.partial(line_kernel, near), out_shape=jax.ShapeD...  325 us

profile of v6, /device:TPU:4, one launch (start us, length us, event | category | flops | bytes accessed | tf_op | source)
XLA Modules:
  0.0 327.3 jit_solution(7656227163260116269)
XLA Ops:
  0.6 324.9 %shard_map.59 = f32[2,48,1008]{2,1,0:T(8,128)} custom-call(f32[504,9192]{1,0:T(8,128)} %t_hbm.1, f32[2,2,48,9192]{3,2,1,0:T(8,128)} %bitcast.11, f32[64]{0:T(128)} %occ_hbm.1, f32[384]{0:T(512)} %vir_hbm.1), custom_call_target="tpu_custom_call" | custom-call | flops 26684743680 | bytes 25590528 | tf_op jit(solution)/shard_map/pallas_call | solution.py:766
  325.5 1.8 slice_bitcast_fusion
